TPU v7x, 32 devices: a whole 2x2x4 slice. The times are simulated.
32 devices in a mesh: row: 4 (over z), col: 8 (over y, x, core).
Axes of the slice: x: 2, y: 2, z: 4, core: 2. Of those that a mesh axis runs over, the one named last changes fastest.
Arguments:
- diag_blocks: float32 [8, 16, 512, 512], P('row', 'col'), may hold values from -4 to 16, as said below
- horizontal: bfloat16 [8, 16, 512, 512], P('row', 'col'), may hold values from -0.125 to 0.125
- vertical: bfloat16 [8, 16, 512, 512], P('row', 'col'), may hold values from -0.125 to 0.125
Outputs:
- red_factor: float32 [8, 8, 512, 512], P('row', 'col')
- black_schur: float32 [8, 8, 512, 512], P('row', 'col')
- black_links: bfloat16 [8, 8, 4, 512, 512], P('row', 'col')
Inputs may be any that keep to these rules, and one draw needn't show every extreme that they name: `diag_blocks`: every block is symmetric and its eigenvalues are at least 1.
All inputs are finite; a program needn't handle non-finite values.
Results may differ from a plain program's by a relative error of at most 0.0054.
Values may be sent and summed in bfloat16 or wider, within the bound.
A program may use at most 128 MiB of HBM per device.

v0:
```python
import jax
import jax.numpy as jnp
from jax import lax
from jax.sharding import PartitionSpec as P


def passed_along(value, axis, by):
    size = lax.axis_size(axis)
    return lax.ppermute(value, axis, [(i, (i + by) % size) for i in range(size)])


def select_colour(blocks, parity):
    grid_rows = blocks.shape[0]
    grid_columns = blocks.shape[1]
    trailing = blocks.shape[2:]
    paired = blocks.reshape((grid_rows // 2, 2, grid_columns // 2, 2) + trailing)
    joined = jnp.stack([paired[:, 0, :, parity], paired[:, 1, :, 1 - parity]], 1)
    return joined.reshape((grid_rows, grid_columns // 2) + trailing)


def combine_rows(even_rows, odd_rows):
    joined = jnp.stack([even_rows, odd_rows], 1)
    return joined.reshape((2 * even_rows.shape[0],) + even_rows.shape[1:])


def transposed(blocks):
    return jnp.swapaxes(blocks, -1, -2)


def gram_term(former, latter):
    return jnp.einsum("rmka,rmkb->rmab", former, latter, preferred_element_type=jnp.float32)


def on_device(diag_blocks, horizontal, vertical):
    edge_column = passed_along(horizontal[:, -1:], "col", 1)
    left_links = jnp.concatenate([edge_column, horizontal[:, :-1]], 1)
    edge_row = passed_along(vertical[-1:], "row", 1)
    upper_links = jnp.concatenate([edge_row, vertical[:-1]], 0)
    couplings = (
        transposed(select_colour(left_links, 0)).astype(jnp.float32),
        transposed(select_colour(upper_links, 0)).astype(jnp.float32),
        select_colour(horizontal, 0).astype(jnp.float32),
        select_colour(vertical, 0).astype(jnp.float32),
    )
    red_factor = jnp.linalg.cholesky(select_colour(diag_blocks, 0))
    results = [
        jax.scipy.linalg.solve_triangular(red_factor, coupling, lower=True)
        for coupling in couplings
    ]
    solved = jnp.stack(results, 2).astype(jnp.bfloat16)
    got_above = passed_along(solved[-1:, :, 3], "row", 1)
    above_down = jnp.concatenate([got_above, solved[:-1, :, 3]], 0)
    got_below = passed_along(solved[:1], "row", -1)
    below_all = jnp.concatenate([solved[1:], got_below], 0)
    got_left = passed_along(solved[1::2, -1:, 2:4], "col", 1)
    left_pair = combine_rows(
        solved[0::2, :, 2:4], jnp.concatenate([got_left, solved[1::2, :-1, 2:4]], 1)
    )
    right_first, right_rest = passed_along((solved[0::2, :1, 0], solved[0::2, :1, 2:4]), "col", -1)
    right_left = combine_rows(
        jnp.concatenate([solved[0::2, 1:, 0], right_first], 1), solved[1::2, :, 0]
    )
    right_pair = combine_rows(
        jnp.concatenate([solved[0::2, 1:, 2:4], right_rest], 1), solved[1::2, :, 2:4]
    )
    below_up = below_all[:, :, 1]
    update = gram_term(above_down, above_down) + gram_term(below_up, below_up)
    update = (
        update
        + gram_term(left_pair[:, :, 0], left_pair[:, :, 0])
        + gram_term(right_left, right_left)
    )
    black_schur = select_colour(diag_blocks, 1) - update
    east_link = -gram_term(right_left, right_pair[:, :, 0])
    south_link = -gram_term(below_up, below_all[:, :, 3])
    southeast = -(
        gram_term(right_left, right_pair[:, :, 1]) + gram_term(below_up, below_all[:, :, 2])
    )
    southwest = -(
        gram_term(left_pair[:, :, 0], left_pair[:, :, 1]) + gram_term(below_up, below_all[:, :, 0])
    )
    black_links = jnp.stack([east_link, south_link, southeast, southwest], 2).astype(jnp.bfloat16)
    return (red_factor, black_schur, black_links)


def solution(mesh):
    in_specs = (
        P("row", "col", None, None),
        P("row", "col", None, None),
        P("row", "col", None, None),
    )
    out_specs = (
        P("row", "col", None, None),
        P("row", "col", None, None),
        P("row", "col", None, None, None),
    )
    return jax.shard_map(
        on_device, mesh=mesh, in_specs=in_specs, out_specs=out_specs, check_vma=False
    )
```

profile of v0, /device:TPU:27, one launch (start us, length us, event | category | flops | bytes accessed | tf_op | source)
XLA Modules:
  0.0 403.3 jit_solution(7077710784273775207)
XLA Ops:
  0.6 2.7 fusion.145
  3.4 1.3 copy.153
  4.7 1.8 collective-permute-start.1
  6.6 5.2 %copy.62 = f32[2,2,512,512]{2,3,1,0:T(8,128)} copy(f32[2,2,512,512]{3,2,1,0:T(8,128)} %param.5) | data formatting | bytes 8388608 | tf_op args[0]
  11.8 4.2 %slice_bitcast_fusion.10 = (f32[1,1,1,512,512]{3,4,2,1,0:T(8,128)}, f32[1,1,1,512,512]{3,4,2,1,0:T(8,128)}, f32[1,1,1,512,512]{3,4,1,2,0:T(8,128)S(1)}, f32[1,1,1,512,512]{3,4,1,2,0:T(8,128)S(1)}) fusion(f32[1,2,1,2,512,512]{4,5,3,2,1,0:T(8,128)} %bitcast.342), kind=kLoop, calls=%fused_computation.110 | loop fusion | bytes 8388608 | tf_op jit(solution)/shard_map/stack;squeeze | solution.py:17
  16.0 1.5 fusion.7
  17.5 2.9 copy.64
  20.3 2.1 fusion.6
  22.4 1.3 copy-done.9
  23.8 23.5 %custom-call.34 = f32[2,1,128,128]{3,2,1,0:T(8,128)S(1)} custom-call(f32[2,1,128,128]{3,2,1,0:T(8,128)S(1)} %cholesky.283), custom_call_target="Cholesky" | custom-call | tf_op jit(solution)/shard_map/jit(cholesky)/cholesky | solution.py:45
  47.3 19.7 %custom-call.35 = f32[2,1,1,128,128]{3,4,2,1,0:T(8,128)S(1)} custom-call(f32[2,1,1,128,128]{4,3,2,1,0:T(8,128)S(1)} %select_bitcast_fusion.2), custom_call_target="InvertDiagBlocksLowerTriangular" | custom-call | tf_op jit(solution)/shard_map/jit(cholesky)/cholesky | solution.py:45
  67.2 1.5 constant_dynamic-update-slice_fusion.3
  68.7 1.5 fusion.47
  70.2 23.7 %custom-call.36 = f32[2,1,128,128]{3,2,1,0:T(8,128)S(1)} custom-call(f32[2,1,128,128]{3,2,1,0:T(8,128)S(1)} %cholesky.287), custom_call_target="Cholesky" | custom-call | tf_op jit(solution)/shard_map/jit(cholesky)/cholesky | solution.py:45
  93.9 19.7 %custom-call.37 = f32[2,1,1,128,128]{3,4,2,1,0:T(8,128)S(1)} custom-call(f32[2,1,1,128,128]{4,3,2,1,0:T(8,128)S(1)} %get-tuple-element.83), custom_call_target="InvertDiagBlocksLowerTriangular" | custom-call | tf_op jit(solution)/shard_map/jit(cholesky)/cholesky | solution.py:45
  114.0 1.6 fusion.49
  115.6 23.5 %custom-call.38 = f32[2,1,128,128]{3,2,1,0:T(8,128)S(1)} custom-call(f32[2,1,128,128]{3,2,1,0:T(8,128)S(1)} %cholesky.292), custom_call_target="Cholesky" | custom-call | tf_op jit(solution)/shard_map/jit(cholesky)/cholesky | solution.py:45
  139.1 20.1 %custom-call.39 = f32[2,1,1,128,128]{3,4,2,1,0:T(8,128)S(1)} custom-call(f32[2,1,1,128,128]{4,3,2,1,0:T(8,128)S(1)} %get-tuple-element.81), custom_call_target="InvertDiagBlocksLowerTriangular" | custom-call | tf_op jit(solution)/shard_map/jit(cholesky)/cholesky | solution.py:45
  159.4 1.5 fusion.51
  161.0 23.5 %custom-call.40 = f32[2,1,128,128]{3,2,1,0:T(8,128)S(1)} custom-call(f32[2,1,128,128]{3,2,1,0:T(8,128)S(1)} %fusion.51), custom_call_target="Cholesky" | custom-call | tf_op jit(solution)/shard_map/jit(cholesky)/cholesky | solution.py:45
  184.8 1.0 copy-done
  185.8 3.6 bitcast_select_fusion
  189.4 10.7 %while.8 = (s32[]{:T(128)}, f32[2,512,512]{2,1,0:T(8,128)S(1)}, s32[4,2]{0,1:T(2,128)S(1)}, f32[4,2,128,128]{3,2,0,1:T(8,128)}, s32[]{:T(128)}) while((s32[]{:T(128)}, f32[2,512,512]{2,1,0:T(8,128)S(1)}, s32[4,2]{0,1:T(2,128)S(1)}, f32[4,2,128,128]{3,2,0,1:T(8,128)}, s32[]{:T(128)}) %tuple.60), condition=%wide.while_cond, body=%wide.while_body.sunk | while | flops 2 | bytes 263777 | solution.py:47
  190.1 2.1 bitcast_dynamic-update-slice_fusion.2
  192.7 2.0 bitcast_dynamic-update-slice_fusion.2
  195.4 2.0 bitcast_dynamic-update-slice_fusion.2
  198.1 2.1 bitcast_dynamic-update-slice_fusion.2
  200.1 79.6 %custom-call.44 = f32[2,4,128,128]{2,3,1,0:T(8,128)S(1)} custom-call(f32[2,4,128,128]{3,2,1,0:T(8,128)} %bitcast.350), custom_call_target="InvertDiagBlocksLowerTriangular" | custom-call | tf_op jit(solution)/shard_map/jit(_solve_triangular)/vmap()/triangular_solve | solution.py:47
  279.7 1.5 slice_bitcast_fusion.17
  283.2 0.7 convolution_subtract_fusion
  284.6 1.1 fusion.35
  287.8 1.6 fusion.113
  290.8 1.1 fusion.44
  292.9 2.3 fusion.142
  295.4 1.6 fusion.146
  297.0 2.3 copy.155
  299.3 1.2 fusion.2
  300.5 1.0 fusion.147
  301.5 1.3 collective-permute-start
  302.8 1.5 copy.154
  304.3 1.5 copy.156
  305.8 1.7 maximum_bitcast_fusion.2
  307.8 0.9 copy-done.7
  311.9 1.1 fusion.41
  313.8 9.9 %collective-permute-done.2 = bf16[1,2,512,512]{2,3,1,0:T(8,128)(2,1)} collective-permute-done((bf16[1,2,512,512]{2,3,1,0:T(8,128)(2,1)}, bf16[1,2,512,512]{2,3,1,0:T(8,128)(2,1)}, u32[]{:S(2)}, u32[]{:S(2)}) %collective-permute-start.2) | collective-permute-done | bytes 1048608 | tf_op jit(solution)/shard_map/ppermute | solution.py:9
  323.7 1.4 maximum_bitcast_fusion.4
  328.5 1.1 fusion.38
  333.0 4.9 %collective-permute-start.4 = (bf16[1,1,2,512,512]{4,3,2,1,0:T(8,128)(2,1)S(1)}, bf16[1,1,2,512,512]{4,3,2,1,0:T(8,128)(2,1)S(1)}, u32[]{:S(2)}, u32[]{:S(2)}) collective-permute-start(bf16[1,1,2,512,512]{4,3,2,1,0:T(8,128)(2,1)S(1)} %copy-done.16), channel_id=1, source_target_pairs={{0,1},{1,2},{2,3},{3,4},{4,5},{5,6},{6,7},{7,0},{8,9},{9,10},{10,1... | collective-permute-start | bytes 3145736 | tf_op jit(solution)/shard_map/ppermute | solution.py:9
  337.9 1.9 fusion.74
  340.2 1.0 copy-done.13
  341.2 1.5 maximum_bitcast_fusion.8
  342.7 12.5 %collective-permute-done.4 = bf16[1,1,2,512,512]{4,3,2,1,0:T(8,128)(2,1)S(1)} collective-permute-done((bf16[1,1,2,512,512]{4,3,2,1,0:T(8,128)(2,1)S(1)}, bf16[1,1,2,512,512]{4,3,2,1,0:T(8,128)(2,1)S(1)}, u32[]{:S(2)}, u32[]{:S(2)}) %collective-permute-start.4) | collective-permute-done | bytes 1048608 | tf_op jit(solution)/shard_map/ppermute | solution.py:9
  355.5 0.8 fusion.87
  356.3 35.2 %collective-permute-done.5 = bf16[1,1,512,512]{3,2,1,0:T(8,128)(2,1)S(1)} collective-permute-done((bf16[1,1,512,512]{3,2,1,0:T(8,128)(2,1)S(1)}, bf16[1,1,512,512]{3,2,1,0:T(8,128)(2,1)S(1)}, u32[]{:S(2)}, u32[]{:S(2)}) %collective-permute-start.5) | collective-permute-done | bytes 524320 | tf_op jit(solution)/shard_map/ppermute | solution.py:9
  391.5 0.8 fusion.32
  392.4 0.8 fusion.148
  393.2 0.8 fusion.58
  393.9 0.8 fusion.34
  394.7 0.8 fusion.66
  395.5 0.8 fusion.52
  396.2 0.8 fusion.33
  397.6 2.5 copy.117
  400.1 0.9 fusion.1
  401.0 1.8 copy.116
  (109 shorter events, 23.2 us)
Async XLA Ops:
  4.7 301.1 %collective-permute-start.1 = (bf16[2,1,512,512]{2,3,1,0:T(8,128)(2,1)}, bf16[2,1,512,512]{2,3,1,0:T(8,128)(2,1)}, u32[]{:S(2)}, u32[]{:S(2)}) collective-permute-start(bf16[2,1,512,512]{2,3,1,0:T(8,128)(2,1)} %copy.153), channel_id=1, source_target_pairs={{0,1},{1,2},{2,3},{3,4},{4,5},{5,6},{6,7},{7,0},{8,9},{9,10},{10,1... | collective-permute-start | bytes 3145736 | tf_op jit(solution)/shard_map/ppermute | solution.py:9
  22.4 1.3 copy-start.9
  184.5 1.3 copy-start
  279.7 6.9 %copy-start.5 = (f32[2,4,128,128]{2,3,1,0:T(8,128)}, f32[2,4,128,128]{2,3,1,0:T(8,128)S(1)}, u32[]{:S(2)}) copy-start(f32[2,4,128,128]{2,3,1,0:T(8,128)S(1)} %custom-call.44) | copy-start | bytes 1572868
  284.6 1.8 copy-start.10
  287.8 2.3 copy-start.6
  290.8 1.9 copy-start.8
  292.7 2.4 copy-start.1
  292.9 2.5 copy-start.3
  295.4 44.8 %collective-permute-start.6 = (bf16[1,1,2,512,512]{4,3,2,1,0:T(8,128)(2,1)}, bf16[1,1,2,512,512]{4,3,2,1,0:T(8,128)(2,1)}, u32[]{:S(2)}, u32[]{:S(2)}) collective-permute-start(bf16[1,1,2,512,512]{4,3,2,1,0:T(8,128)(2,1)} %get-tuple-element.62), channel_id=1, source_target_pairs={{0,7},{1,0},{2,1},{3,2},{4,3},{5,4},{6,5},{7,6},{8,15},{9,8},{10,9... | collective-permute-start | bytes 3145736 | tf_op jit(solution)/shard_map/ppermute | solution.py:9
  299.3 24.4 %collective-permute-start.2 = (bf16[1,2,512,512]{2,3,1,0:T(8,128)(2,1)}, bf16[1,2,512,512]{2,3,1,0:T(8,128)(2,1)}, u32[]{:S(2)}, u32[]{:S(2)}) collective-permute-start(bf16[1,2,512,512]{2,3,1,0:T(8,128)(2,1)} %copy.155), channel_id=1, source_target_pairs={{0,8},{8,16},{16,24},{24,0},{1,9},{9,17},{17,25},{25,1},{2,10},{10... | collective-permute-start | bytes 3145736 | tf_op jit(solution)/shard_map/ppermute | solution.py:9
  300.5 2.3 copy-start.11
  301.5 36.4 %collective-permute-start = (bf16[1,1,512,512]{3,2,0,1:T(8,128)(2,1)}, bf16[1,1,512,512]{3,2,0,1:T(8,128)(2,1)}, u32[]{:S(2)}, u32[]{:S(2)}) collective-permute-start(bf16[1,1,512,512]{3,2,0,1:T(8,128)(2,1)} %get-tuple-element.78), channel_id=1, source_target_pairs={{0,8},{8,16},{16,24},{24,0},{1,9},{9,17},{17,25},{25,1},{2,10},{10... | collective-permute-start | bytes 1572872 | tf_op jit(solution)/shard_map/ppermute | solution.py:9
  307.6 1.0 copy-start.7
  329.7 1.2 copy-start.2
  329.7 1.5 copy-start.4
  331.8 1.2 copy-start.16
  331.8 6.1 %copy-start.17 = (bf16[1,1,512,512]{3,2,0,1:T(8,128)(2,1)S(1)}, bf16[1,1,512,512]{3,2,0,1:T(8,128)(2,1)}, u32[]{:S(2)}) copy-start(bf16[1,1,512,512]{3,2,0,1:T(8,128)(2,1)} %get-tuple-element.79) | copy-start | bytes 1572868
  332.1 60.2 %collective-permute-start.3 = (bf16[1,1,4,512,512]{4,3,0,2,1:T(8,128)(2,1)S(1)}, bf16[1,1,4,512,512]{4,3,0,2,1:T(8,128)(2,1)S(1)}, u32[]{:S(2)}, u32[]{:S(2)}) collective-permute-start(bf16[1,1,4,512,512]{4,3,0,2,1:T(8,128)(2,1)S(1)} %get-tuple-element.56), channel_id=1, source_target_pairs={{0,24},{8,0},{16,8},{24,16},{1,25},{9,1},{17,9},{25,17},{2,26},{10... | collective-permute-start | bytes 6291464 | tf_op jit(solution)/shard_map/ppermute | solution.py:9
  333.0 22.3 %collective-permute-start.4 = (bf16[1,1,2,512,512]{4,3,2,1,0:T(8,128)(2,1)S(1)}, bf16[1,1,2,512,512]{4,3,2,1,0:T(8,128)(2,1)S(1)}, u32[]{:S(2)}, u32[]{:S(2)}) collective-permute-start(bf16[1,1,2,512,512]{4,3,2,1,0:T(8,128)(2,1)S(1)} %copy-done.16), channel_id=1, source_target_pairs={{0,1},{1,2},{2,3},{3,4},{4,5},{5,6},{6,7},{7,0},{8,9},{9,10},{10,1... | collective-permute-start | bytes 3145736 | tf_op jit(solution)/shard_map/ppermute | solution.py:9
  340.0 1.2 copy-start.13
  340.0 51.5 %collective-permute-start.5 = (bf16[1,1,512,512]{3,2,1,0:T(8,128)(2,1)S(1)}, bf16[1,1,512,512]{3,2,1,0:T(8,128)(2,1)S(1)}, u32[]{:S(2)}, u32[]{:S(2)}) collective-permute-start(bf16[1,1,512,512]{3,2,1,0:T(8,128)(2,1)S(1)} %slice.292), channel_id=1, source_target_pairs={{0,7},{1,0},{2,1},{3,2},{4,3},{5,4},{6,5},{7,6},{8,15},{9,8},{10,9... | collective-permute-start | bytes 1572872 | tf_op jit(solution)/shard_map/ppermute | solution.py:9
  341.2 14.0 %copy-start.12 = (bf16[1,1,1,2,512,512]{5,4,3,2,1,0:T(8,128)(2,1)S(1)}, bf16[1,1,1,2,512,512]{5,4,3,2,1,0:T(8,128)(2,1)}, u32[]{:S(2)}) copy-start(bf16[1,1,1,2,512,512]{5,4,3,2,1,0:T(8,128)(2,1)} %get-tuple-element.63) | copy-start | bytes 3145732
  397.6 2.5 copy-start.14
  397.6 2.5 copy-start.15
where the time goes:
time: 411 us; the launch traced here: 403 us
  other arithmetic  252 us (61%)
  waiting for transfers between devices  57.7 us (14%)
  local copies, waits for them, and re-layouts  47.4 us (12%)
  matrix products  36.4 us (9%)
  starting transfers between devices  8.25 us (2%)
    another operation x16, other arithmetic, on_device(): red_factor = jnp.linalg.cholesky(select_colour(diag_blocks, 0))  154 us
    another operation x4, other arithmetic, on_device(): jax.scipy.linalg.solve_triangular(red_factor, coupling, lower=True)  83.2 us
    ppermute x7, waiting for transfers between devices, passed_along(): lax.ppermute(value, axis, [(i, (i + by) % size) for i in range(size)])  57.7 us
    unnamed x43, local copies, waits for them, and re-layouts  22 us
    another operation x28, matrix products, on_device(): jax.scipy.linalg.solve_triangular(red_factor, coupling, lower=True)  20.7 us
    another operation x13, local copies, waits for them, and re-layouts, on_device(): jax.scipy.linalg.solve_triangular(red_factor, coupling, lower=True)  10.7 us
    dot_general x10, matrix products, gram_term(): jnp.einsum('rmka,rmkb->rmab', former, latter, preferred_element_type=jnp....  8.94 us
    ppermute x7, starting transfers between devices, passed_along(): lax.ppermute(value, axis, [(i, (i + by) % size) for i in range(size)])  8.25 us
  transfers between devices with their start and end apart: 7, of which 3 were waited for; matrix products, arithmetic and copies ran while one was open for 78% of the time, Pallas kernels for 0%

commit v1 on v0

--- a/solution.py
+++ b/solution.py
@@ -1,7 +1,126 @@
+import functools
+
 import jax
 import jax.numpy as jnp
 from jax import lax
+from jax.experimental import pallas as pl
+from jax.experimental.pallas import tpu as pltpu
 from jax.sharding import PartitionSpec as P
+
+PANEL = 128
+STRIP = 8
+VMEM = pl.BlockSpec(memory_space=pltpu.VMEM)
+
+
+def split(value):
+    high = value.astype(jnp.bfloat16)
+    low = (value - high.astype(jnp.float32)).astype(jnp.bfloat16)
+    return high, low
+
+
+def product(left, right):
+    dot = functools.partial(jnp.dot, preferred_element_type=jnp.float32)
+    (lh, ll), (rh, rl) = left, right
+    return dot(lh, rh) + (dot(lh, rl) + dot(ll, rh))
+
+
+def factor_diagonal(work, count):
+    lane = lax.broadcasted_iota(jnp.int32, (STRIP, PANEL), 1)
+    sub = lax.broadcasted_iota(jnp.int32, (STRIP, PANEL), 0)
+    sub_wide = lax.broadcasted_iota(jnp.int32, (STRIP, 2 * PANEL), 0)
+
+    def strip(b, carry):
+        start = pl.multiple_of(b * STRIP, STRIP)
+        rows = [work[m, pl.ds(start, STRIP), :] for m in range(count)]
+        columns = [
+            [
+                jnp.take_along_axis(rows[m][:, :PANEL], jnp.full_like(lane, start + c), axis=1)
+                for c in range(STRIP)
+            ]
+            for m in range(count)
+        ]
+        for j in range(STRIP):
+            for m in range(count):
+                column = columns[m][j]
+                pivot = jnp.broadcast_to(column[j : j + 1], column.shape)
+                root = lax.rsqrt(pivot)
+                square = root * root
+                below = jnp.where(sub > j, column, 0.0)
+                for c in range(j + 1, STRIP):
+                    across = jnp.broadcast_to(columns[m][c][j : j + 1], column.shape)
+                    columns[m][c] = columns[m][c] - (below * across) * square
+                row = jnp.broadcast_to(rows[m][j : j + 1], rows[m].shape)
+                wide_below = jnp.concatenate([below * square] * 2, 1)
+                wide_root = jnp.concatenate([root] * 2, 1)
+                rows[m] = jnp.where(sub_wide == j, row * wide_root, rows[m] - wide_below * row)
+        for m in range(count):
+            work[m, pl.ds(start, STRIP), :] = rows[m]
+            high = rows[m].astype(jnp.bfloat16).astype(jnp.float32)
+            low = rows[m] - high
+            after = lane >= start + STRIP
+            left_high = jnp.where(after, high[:, :PANEL], 0.0)
+            left_low = jnp.where(after, low[:, :PANEL], 0.0)
+            left = jnp.concatenate([left_high, left_high, left_low, left_low], 0)
+            right = jnp.concatenate([high, low, high, low], 0)
+            work[m] = work[m] - lax.dot_general(
+                left.T.astype(jnp.bfloat16),
+                right.astype(jnp.bfloat16),
+                (((1,), (0,)), ((), ())),
+                preferred_element_type=jnp.float32,
+            )
+        return carry
+
+    lax.fori_loop(0, PANEL // STRIP, strip, 0)
+
+
+def factor_kernel(diag, factor, inverse, blocks, work):
+    count, order = diag.shape[0], diag.shape[1]
+    row = lax.broadcasted_iota(jnp.int32, (PANEL, PANEL), 0)
+    col = lax.broadcasted_iota(jnp.int32, (PANEL, PANEL), 1)
+    eye = jnp.where(row == col, 1.0, 0.0).astype(jnp.float32)
+    blocks[...] = diag[...]
+    inverse[...] = jnp.zeros_like(inverse)
+    factor[...] = jnp.zeros_like(factor)
+    for start in range(0, order, PANEL):
+        stop = start + PANEL
+        here = slice(start, stop)
+        for m in range(count):
+            work[m, :, :PANEL] = blocks[m, here, here]
+            work[m, :, PANEL:] = eye
+        factor_diagonal(work, count)
+        for m in range(count):
+            upper = jnp.where(col >= row, work[m, :, :PANEL], 0.0)
+            factor[m, here, here] = upper.T
+            small = jnp.where(col <= row, work[m, :, PANEL:], 0.0)
+            small_parts = split(small)
+            if start:
+                inverse[m, here, :start] = product(small_parts, split(inverse[m, here, :start]))
+            inverse[m, here, here] = small
+            if stop < order:
+                across = product(small_parts, split(blocks[m, here, stop:]))
+                down = across.T
+                factor[m, stop:, here] = down
+                down_parts = split(down)
+                blocks[m, stop:, stop:] -= product(down_parts, split(across))
+                inverse[m, stop:, :stop] -= product(down_parts, split(inverse[m, here, :stop]))
+
+
+def factored(diag):
+    shape = jax.ShapeDtypeStruct(diag.shape, jnp.float32)
+    return pl.pallas_call(
+        factor_kernel,
+        out_shape=(shape, shape),
+        in_specs=[VMEM],
+        out_specs=(VMEM, VMEM),
+        scratch_shapes=[
+            pltpu.VMEM(diag.shape, jnp.float32),
+            pltpu.VMEM((diag.shape[0], PANEL, 2 * PANEL), jnp.float32),
+        ],
+        compiler_params=pltpu.CompilerParams(vmem_limit_bytes=40 * 2**20),
+        cost_estimate=pl.CostEstimate(
+            flops=20_000_000_000, bytes_accessed=3 * diag.size * 4, transcendentals=0
+        ),
+    )(diag)
 
 
 def passed_along(value, axis, by):
@@ -31,23 +150,31 @@
     return jnp.einsum("rmka,rmkb->rmab", former, latter, preferred_element_type=jnp.float32)
 
 
+def solve(inverse, coupling, axes):
+    high, low = split(inverse)
+    dot = functools.partial(jnp.einsum, axes, preferred_element_type=jnp.float32)
+    return dot(high, coupling) + dot(low, coupling)
+
+
 def on_device(diag_blocks, horizontal, vertical):
+    rows, half = diag_blocks.shape[0], diag_blocks.shape[1] // 2
+    block = diag_blocks.shape[2:]
     edge_column = passed_along(horizontal[:, -1:], "col", 1)
     left_links = jnp.concatenate([edge_column, horizontal[:, :-1]], 1)
     edge_row = passed_along(vertical[-1:], "row", 1)
     upper_links = jnp.concatenate([edge_row, vertical[:-1]], 0)
-    couplings = (
-        transposed(select_colour(left_links, 0)).astype(jnp.float32),
-        transposed(select_colour(upper_links, 0)).astype(jnp.float32),
-        select_colour(horizontal, 0).astype(jnp.float32),
-        select_colour(vertical, 0).astype(jnp.float32),
-    )
-    red_factor = jnp.linalg.cholesky(select_colour(diag_blocks, 0))
-    results = [
-        jax.scipy.linalg.solve_triangular(red_factor, coupling, lower=True)
-        for coupling in couplings
-    ]
-    solved = jnp.stack(results, 2).astype(jnp.bfloat16)
+    red_factor, inverse = factored(select_colour(diag_blocks, 0).reshape((-1,) + block))
+    inverse = inverse.reshape((rows, half) + block)
+    solved = jnp.stack(
+        [
+            solve(inverse, select_colour(left_links, 0), "rmab,rmcb->rmac"),
+            solve(inverse, select_colour(upper_links, 0), "rmab,rmcb->rmac"),
+            solve(inverse, select_colour(horizontal, 0), "rmab,rmbc->rmac"),
+            solve(inverse, select_colour(vertical, 0), "rmab,rmbc->rmac"),
+        ],
+        2,
+    ).astype(jnp.bfloat16)
+    red_factor = red_factor.reshape((rows, half) + block)
     got_above = passed_along(solved[-1:, :, 3], "row", 1)
     above_down = jnp.concatenate([got_above, solved[:-1, :, 3]], 0)
     got_below = passed_along(solved[:1], "row", -1)

time: 411 us -> 129 us (0.31); the launches traced: 403 us -> 127 us
  other arithmetic: 252 us -> 2.79 us
  local copies, waits for them, and re-layouts: 47.4 us -> 6.69 us
  Pallas kernels: 0 us -> 31.6 us
  matrix products: 36.4 us -> 15.1 us
    another operation x29 -> x3, other arithmetic: 240 us -> 0.85 us  [the longest x1 0.57 us: on_device(): jnp.stack([solve(inverse, select_colour(left_links, 0), 'rmab,rmcb->rmac'...]
    pallas_call x0 -> x1, Pallas kernels: none -> 31.6 us  [factored(): pl.pallas_call(factor_kernel, out_shape=(shape, shape), in_specs=[VMEM],...]
    another operation x34 -> x0, matrix products: 27.5 us -> none  [the longest x28 20.7 us: on_device(): jax.scipy.linalg.solve_triangular(red_factor, coupling, lower=True)]
    unnamed x43 -> x7, local copies, waits for them, and re-layouts: 22 us -> 3.58 us
    another operation x17 -> x0, local copies, waits for them, and re-layouts: 11 us -> none  [the longest x13 10.7 us: on_device(): jax.scipy.linalg.solve_triangular(red_factor, coupling, lower=True)]
    dot_general x0 -> x8, matrix products: none -> 5.88 us  [solve(): return dot(high, coupling) + dot(low, coupling)]
    another operation x5, local copies, waits for them, and re-layouts: 5.82 us -> 0.73 us  [select_colour(): jnp.stack([paired[:, 0, :, parity], paired[:, 1, :, 1 - parity]], 1)]
  transfers between devices with their start and end apart: 7 -> 7, of which waited for: 3 -> 2; matrix products, arithmetic and copies ran while one was open for 78% -> 7% of each run, Pallas kernels for 0% -> 25%
where the time goes in v1:
time: 129 us; the launch traced here: 127 us
  waiting for transfers between devices  61.4 us (48%)
  Pallas kernels  31.6 us (24%)
  matrix products  15.1 us (12%)
  starting transfers between devices  8.9 us (7%)
  local copies, waits for them, and re-layouts  6.69 us (5%)
  other arithmetic  2.79 us (2%)
    ppermute x7, waiting for transfers between devices, passed_along(): lax.ppermute(value, axis, [(i, (i + by) % size) for i in range(size)])  61.4 us
    pallas_call x1, Pallas kernels, factored(): pl.pallas_call(factor_kernel, out_shape=(shape, shape), in_specs=[VMEM],...  31.6 us
    dot_general x10, matrix products, gram_term(): jnp.einsum('rmka,rmkb->rmab', former, latter, preferred_element_type=jnp....  9.18 us
    ppermute x7, starting transfers between devices, passed_along(): lax.ppermute(value, axis, [(i, (i + by) % size) for i in range(size)])  8.9 us
    dot_general x8, matrix products, solve(): return dot(high, coupling) + dot(low, coupling)  5.88 us
    unnamed x7, local copies, waits for them, and re-layouts  3.58 us
  transfers between devices with their start and end apart: 7, of which 2 were waited for; matrix products, arithmetic and copies ran while one was open for 7% of the time, Pallas kernels for 25%

profile of v1, /device:TPU:27, one launch (start us, length us, event | category | flops | bytes accessed | tf_op | source)
XLA Modules:
  0.0 127.3 jit_solution(2078239661493779669)
XLA Ops:
  0.6 0.0 copy-start
  0.6 1.8 %fusion.51 = (bf16[2,1,512,512]{3,2,1,0:T(8,128)(2,1)S(1)}, bf16[2,1,512,512]{3,2,1,0:T(8,128)(2,1)S(1)}) fusion(bf16[2,2,512,512]{3,2,1,0:T(8,128)(2,1)} %param.4), kind=kLoop, calls=%fused_computation.101 | loop fusion | bytes 4194304 | tf_op jit(solution)/shard_map/slice | solution.py:162
  2.5 0.0 copy-start.2
  2.5 1.8 %collective-permute-start.1 = (bf16[2,1,512,512]{3,2,1,0:T(8,128)(2,1)S(1)}, bf16[2,1,512,512]{3,2,1,0:T(8,128)(2,1)S(1)}, u32[]{:S(2)}, u32[]{:S(2)}) collective-permute-start(bf16[2,1,512,512]{3,2,1,0:T(8,128)(2,1)S(1)} %get-tuple-element.24), channel_id=1, source_target_pairs={{0,1},{1,2},{2,3},{3,4},{4,5},{5,6},{6,7},{7,0},{8,9},{9,10},{10,1... | collective-permute-start | bytes 3145736 | tf_op jit(solution)/shard_map/ppermute | solution.py:128
  4.3 0.0 copy-done
  4.3 0.1 fusion.52
  4.5 0.1 collective-permute-start.2
  4.5 0.2 copy-done.2
  4.8 0.5 slice_bitcast_fusion.10
  5.2 0.2 maximum_bitcast_fusion.diag
  5.4 31.6 %shard_map.58 = (f32[2,512,512]{2,1,0:T(8,128)}, f32[2,512,512]{2,1,0:T(8,128)S(1)}) custom-call(f32[2,512,512]{2,1,0:T(8,128)S(1)} %maximum_bitcast_fusion.diag), custom_call_target="tpu_custom_call" | custom-call | flops 20000000000 | bytes 6291456 | tf_op jit(solution)/shard_map/pallas_call | solution.py:110
  37.0 0.3 subtract_convert_fusion
  37.3 0.1 slice_bitcast_fusion.26
  37.4 0.0 copy-start.1
  37.4 0.7 fusion.30
  38.1 0.9 copy-done.1
  39.0 0.1 slice_bitcast_fusion.18
  39.0 0.7 fusion.27
  39.7 0.7 fusion.3
  40.5 0.7 add_convert_fusion.3
  41.2 0.0 collective-permute-done.1
  41.2 0.2 maximum_bitcast_fusion.2
  41.4 0.1 slice_bitcast_fusion.22
  41.5 0.8 fusion.29
  42.3 0.7 add_convert_fusion.2
  43.0 0.0 collective-permute-done.2
  43.0 0.2 maximum_bitcast_fusion.3
  43.2 0.1 slice_bitcast_fusion.20
  43.3 0.7 fusion.28
  44.1 0.7 fusion.2
  44.8 0.6 pad_maximum_fusion
  45.4 0.3 fusion.50
  45.7 1.2 collective-permute-start.3
  46.9 0.3 fusion.49
  47.2 0.1 collective-permute-start.6
  47.3 0.1 slice_bitcast_fusion.24
  47.3 3.0 %collective-permute-start = (bf16[1,1,512,512]{3,2,1,0:T(8,128)(2,1)S(1)}, bf16[1,1,512,512]{3,2,1,0:T(8,128)(2,1)S(1)}, u32[]{:S(2)}, u32[]{:S(2)}) collective-permute-start(bf16[1,1,512,512]{3,2,1,0:T(8,128)(2,1)S(1)} %get-tuple-element.36), channel_id=1, source_target_pairs={{0,8},{8,16},{16,24},{24,0},{1,9},{9,17},{17,25},{25,1},{2,10},{10... | collective-permute-start | bytes 1572872 | tf_op jit(solution)/shard_map/ppermute | solution.py:128
  50.4 2.0 %collective-permute-start.4 = (bf16[1,1,2,512,512]{4,3,2,1,0:T(8,128)(2,1)S(1)}, bf16[1,1,2,512,512]{4,3,2,1,0:T(8,128)(2,1)S(1)}, u32[]{:S(2)}, u32[]{:S(2)}) collective-permute-start(bf16[1,1,2,512,512]{4,3,2,1,0:T(8,128)(2,1)S(1)} %get-tuple-element.20), channel_id=1, source_target_pairs={{0,1},{1,2},{2,3},{3,4},{4,5},{5,6},{6,7},{7,0},{8,9},{9,10},{10,1... | collective-permute-start | bytes 3145736 | tf_op jit(solution)/shard_map/ppermute | solution.py:128
  52.4 53.7 %collective-permute-done = bf16[1,1,512,512]{3,2,1,0:T(8,128)(2,1)S(1)} collective-permute-done((bf16[1,1,512,512]{3,2,1,0:T(8,128)(2,1)S(1)}, bf16[1,1,512,512]{3,2,1,0:T(8,128)(2,1)S(1)}, u32[]{:S(2)}, u32[]{:S(2)}) %collective-permute-start) | collective-permute-done | bytes 524320 | tf_op jit(solution)/shard_map/ppermute | solution.py:128
  106.0 0.8 fusion.23
  106.8 0.1 slice_bitcast_fusion.16
  106.9 0.7 collective-permute-start.5
  107.6 0.0 collective-permute-done.6
  107.6 0.2 maximum_bitcast_fusion.5
  107.8 0.0 collective-permute-done.4
  107.8 0.2 maximum_bitcast_fusion.4
  108.0 0.8 fusion.26
  108.7 7.7 %collective-permute-done.5 = bf16[1,1,512,512]{3,2,1,0:T(8,128)(2,1)S(1)} collective-permute-done((bf16[1,1,512,512]{3,2,1,0:T(8,128)(2,1)S(1)}, bf16[1,1,512,512]{3,2,1,0:T(8,128)(2,1)S(1)}, u32[]{:S(2)}, u32[]{:S(2)}) %collective-permute-start.5) | collective-permute-done | bytes 524320 | tf_op jit(solution)/shard_map/ppermute | solution.py:128
  116.4 0.8 fusion.4
  117.2 0.0 collective-permute-done.3
  117.2 0.1 fusion.14
  117.3 0.8 fusion.53
  118.1 0.8 fusion.11
  118.9 0.8 fusion.6
  119.7 0.8 fusion.19
  120.4 0.8 fusion.7
  121.2 0.8 fusion.5
  122.0 0.6 pad_maximum_fusion.1
  122.6 2.5 %copy.25 = bf16[2,1,4,512,512]{4,3,2,1,0:T(8,128)(2,1)} copy(bf16[2,1,4,512,512]{4,3,0,2,1:T(8,128)(2,1)S(1)} %pad_maximum_fusion.1) | data formatting | bytes 8388608
  125.0 2.3 %fusion.1 = f32[2,1,512,512]{3,2,1,0:T(8,128)} fusion(f32[1,1,1,512,512]{4,3,2,1,0:T(8,128)S(1)} %get-tuple-element.15, f32[1,1,1,512,512]{4,3,2,1,0:T(8,128)S(1)} %get-tuple-element.14, f32[2,512,512]{2,1,0:T(8,128)S(1)} %fusion.26, f32[2,512,512]{2,1,0:T(8,128)S(1)} %fusion.23, f32[2,512,512]{2,1,0:T(8,128)S(1)} %fusion.53, ...), kind=kOutput, calls=%fused_computation.11 | convolution fusion | flops 540016640 | bytes 11534336 | tf_op jit(solution)/shard_map/rmka,rmkb->rmab/dot_general | solution.py:150
Async XLA Ops:
  0.6 3.7 %copy-start = (bf16[2,2,512,512]{3,2,1,0:T(8,128)(2,1)S(1)}, bf16[2,2,512,512]{3,2,1,0:T(8,128)(2,1)}, u32[]{:S(2)}) copy-start(bf16[2,2,512,512]{3,2,1,0:T(8,128)(2,1)} %param.5) | copy-start | bytes 6291460
  2.5 2.3 %copy-start.2 = (f32[2,2,512,512]{3,2,1,0:T(8,128)S(1)}, f32[2,2,512,512]{3,2,1,0:T(8,128)}, u32[]{:S(2)}) copy-start(f32[2,2,512,512]{3,2,1,0:T(8,128)} %param.3) | copy-start | bytes 12582916
  2.5 38.7 %collective-permute-start.1 = (bf16[2,1,512,512]{3,2,1,0:T(8,128)(2,1)S(1)}, bf16[2,1,512,512]{3,2,1,0:T(8,128)(2,1)S(1)}, u32[]{:S(2)}, u32[]{:S(2)}) collective-permute-start(bf16[2,1,512,512]{3,2,1,0:T(8,128)(2,1)S(1)} %get-tuple-element.24), channel_id=1, source_target_pairs={{0,1},{1,2},{2,3},{3,4},{4,5},{5,6},{6,7},{7,0},{8,9},{9,10},{10,1... | collective-permute-start | bytes 3145736 | tf_op jit(solution)/shard_map/ppermute | solution.py:128
  4.5 38.6 %collective-permute-start.2 = (bf16[1,2,512,512]{3,2,1,0:T(8,128)(2,1)S(1)}, bf16[1,2,512,512]{3,2,1,0:T(8,128)(2,1)S(1)}, u32[]{:S(2)}, u32[]{:S(2)}) collective-permute-start(bf16[1,2,512,512]{3,2,1,0:T(8,128)(2,1)S(1)} %get-tuple-element.28), channel_id=1, source_target_pairs={{0,8},{8,16},{16,24},{24,0},{1,9},{9,17},{17,25},{25,1},{2,10},{10... | collective-permute-start | bytes 3145736 | tf_op jit(solution)/shard_map/ppermute | solution.py:128
  37.4 1.6 %copy-start.1 = (bf16[2,2,512,512]{3,2,1,0:T(8,128)(2,1)S(1)}, bf16[2,2,512,512]{3,2,1,0:T(8,128)(2,1)}, u32[]{:S(2)}) copy-start(bf16[2,2,512,512]{3,2,1,0:T(8,128)(2,1)} %param.4) | copy-start | bytes 6291460
  45.7 71.5 %collective-permute-start.3 = (bf16[1,1,4,512,512]{4,3,0,2,1:T(8,128)(2,1)S(1)}, bf16[1,1,4,512,512]{4,3,0,2,1:T(8,128)(2,1)S(1)}, u32[]{:S(2)}, u32[]{:S(2)}) collective-permute-start(bf16[1,1,4,512,512]{4,3,0,2,1:T(8,128)(2,1)S(1)} %get-tuple-element.12), channel_id=1, source_target_pairs={{0,24},{8,0},{16,8},{24,16},{1,25},{9,1},{17,9},{25,17},{2,26},{10... | collective-permute-start | bytes 6291464 | tf_op jit(solution)/shard_map/ppermute | solution.py:128
  47.2 60.4 %collective-permute-start.6 = (bf16[1,1,2,512,512]{4,3,2,1,0:T(8,128)(2,1)S(1)}, bf16[1,1,2,512,512]{4,3,2,1,0:T(8,128)(2,1)S(1)}, u32[]{:S(2)}, u32[]{:S(2)}) collective-permute-start(bf16[1,1,2,512,512]{4,3,2,1,0:T(8,128)(2,1)S(1)} %get-tuple-element.18), channel_id=1, source_target_pairs={{0,7},{1,0},{2,1},{3,2},{4,3},{5,4},{6,5},{7,6},{8,15},{9,8},{10,9... | collective-permute-start | bytes 3145736 | tf_op jit(solution)/shard_map/ppermute | solution.py:128
  47.3 58.7 %collective-permute-start = (bf16[1,1,512,512]{3,2,1,0:T(8,128)(2,1)S(1)}, bf16[1,1,512,512]{3,2,1,0:T(8,128)(2,1)S(1)}, u32[]{:S(2)}, u32[]{:S(2)}) collective-permute-start(bf16[1,1,512,512]{3,2,1,0:T(8,128)(2,1)S(1)} %get-tuple-element.36), channel_id=1, source_target_pairs={{0,8},{8,16},{16,24},{24,0},{1,9},{9,17},{17,25},{25,1},{2,10},{10... | collective-permute-start | bytes 1572872 | tf_op jit(solution)/shard_map/ppermute | solution.py:128
  50.4 57.4 %collective-permute-start.4 = (bf16[1,1,2,512,512]{4,3,2,1,0:T(8,128)(2,1)S(1)}, bf16[1,1,2,512,512]{4,3,2,1,0:T(8,128)(2,1)S(1)}, u32[]{:S(2)}, u32[]{:S(2)}) collective-permute-start(bf16[1,1,2,512,512]{4,3,2,1,0:T(8,128)(2,1)S(1)} %get-tuple-element.20), channel_id=1, source_target_pairs={{0,1},{1,2},{2,3},{3,4},{4,5},{5,6},{6,7},{7,0},{8,9},{9,10},{10,1... | collective-permute-start | bytes 3145736 | tf_op jit(solution)/shard_map/ppermute | solution.py:128
  106.9 9.6 %collective-permute-start.5 = (bf16[1,1,512,512]{3,2,1,0:T(8,128)(2,1)S(1)}, bf16[1,1,512,512]{3,2,1,0:T(8,128)(2,1)S(1)}, u32[]{:S(2)}, u32[]{:S(2)}) collective-permute-start(bf16[1,1,512,512]{3,2,1,0:T(8,128)(2,1)S(1)} %get-tuple-element.34), channel_id=1, source_target_pairs={{0,7},{1,0},{2,1},{3,2},{4,3},{5,4},{6,5},{7,6},{8,15},{9,8},{10,9... | collective-permute-start | bytes 1572872 | tf_op jit(solution)/shard_map/ppermute | solution.py:128

commit v2 on v1

--- a/solution.py
+++ b/solution.py
@@ -73,12 +73,17 @@
     lax.fori_loop(0, PANEL // STRIP, strip, 0)
 
 
-def factor_kernel(diag, factor, inverse, blocks, work):
-    count, order = diag.shape[0], diag.shape[1]
+def triangle(order):
+    return [(p, q) for p in range(order // PANEL) for q in range(p + 1)]
+
+
+def factor_kernel(diag, factor, packed, inverse, blocks, work):
+    count, order = diag.shape[0], diag.shape[2]
     row = lax.broadcasted_iota(jnp.int32, (PANEL, PANEL), 0)
     col = lax.broadcasted_iota(jnp.int32, (PANEL, PANEL), 1)
     eye = jnp.where(row == col, 1.0, 0.0).astype(jnp.float32)
-    blocks[...] = diag[...]
+    for m in range(count):
+        blocks[m] = diag[m, m]
     inverse[...] = jnp.zeros_like(inverse)
     factor[...] = jnp.zeros_like(factor)
     for start in range(0, order, PANEL):
@@ -105,22 +110,84 @@
                 inverse[m, stop:, :stop] -= product(down_parts, split(inverse[m, here, :stop]))
 
 
+    for m in range(count):
+        for n, (p, q) in enumerate(triangle(order)):
+            tile = inverse[m, p * PANEL : (p + 1) * PANEL, q * PANEL : (q + 1) * PANEL]
+            packed[m, 0, n], packed[m, 1, n] = split(tile)
+
+
 def factored(diag):
-    shape = jax.ShapeDtypeStruct(diag.shape, jnp.float32)
+    count, order = diag.shape[0], diag.shape[2]
+    whole = (count, order, order)
+    packed = (count, 2, len(triangle(order)), PANEL, PANEL)
     return pl.pallas_call(
         factor_kernel,
-        out_shape=(shape, shape),
+        out_shape=(
+            jax.ShapeDtypeStruct(whole, jnp.float32),
+            jax.ShapeDtypeStruct(packed, jnp.bfloat16),
+        ),
         in_specs=[VMEM],
         out_specs=(VMEM, VMEM),
         scratch_shapes=[
-            pltpu.VMEM(diag.shape, jnp.float32),
-            pltpu.VMEM((diag.shape[0], PANEL, 2 * PANEL), jnp.float32),
+            pltpu.VMEM(whole, jnp.float32),
+            pltpu.VMEM(whole, jnp.float32),
+            pltpu.VMEM((count, PANEL, 2 * PANEL), jnp.float32),
         ],
         compiler_params=pltpu.CompilerParams(vmem_limit_bytes=40 * 2**20),
         cost_estimate=pl.CostEstimate(
             flops=20_000_000_000, bytes_accessed=3 * diag.size * 4, transcendentals=0
         ),
     )(diag)
+
+
+def apply_inverse(packed, m, couplings, full, out):
+    order = full.shape[1]
+    group = 2 * PANEL
+    for p in range(order // PANEL - 1):
+        corner = (slice(p * PANEL, (p + 1) * PANEL), slice((p + 1) * PANEL, (p + 2) * PANEL))
+        full[0, corner[0], corner[1]] = jnp.zeros((PANEL, PANEL), jnp.bfloat16)
+        full[1, corner[0], corner[1]] = jnp.zeros((PANEL, PANEL), jnp.bfloat16)
+    for n, (p, q) in enumerate(triangle(order)):
+        for part in range(2):
+            full[part, p * PANEL : (p + 1) * PANEL, q * PANEL : (q + 1) * PANEL] = packed[m, part, n]
+    for start in range(0, order, group):
+        stop = start + group
+        high, low = full[0, start:stop, :stop], full[1, start:stop, :stop]
+        for d, coupling in enumerate(couplings):
+            right = coupling[:, :stop] if d < 2 else coupling[:stop, :]
+            axes = (((1,), (1 if d < 2 else 0,)), ((), ()))
+            dot = functools.partial(
+                lax.dot_general, dimension_numbers=axes, preferred_element_type=jnp.float32
+            )
+            out[d, start:stop, :] = (dot(high, right) + dot(low, right)).astype(jnp.bfloat16)
+
+
+def own_kernel(packed, edge_left, edge_up, horizontal, vertical, out, full):
+    first = (edge_left.at[0, 0], edge_up.at[0, 0], horizontal.at[0, 0], vertical.at[0, 0])
+    second = (horizontal.at[1, 0], vertical.at[0, 1], horizontal.at[1, 1], vertical.at[1, 1])
+    apply_inverse(packed, 0, first, full, out.at[0, 0])
+    apply_inverse(packed, 1, second, full, out.at[1, 0])
+
+
+def below_kernel(packed, left, up, right, out, full):
+    couplings = (left.at[0, 0], up.at[1, 0], right.at[0], right.at[1])
+    apply_inverse(packed, 0, couplings, full, out.at[0, 0])
+
+
+def solved_with(kernel, count, operands):
+    order = operands[-1].shape[-1]
+    flops = 12 * count * order**3
+    return pl.pallas_call(
+        kernel,
+        out_shape=jax.ShapeDtypeStruct((count, 1, 4, order, order), jnp.bfloat16),
+        in_specs=[VMEM] * len(operands),
+        out_specs=VMEM,
+        scratch_shapes=[pltpu.VMEM((2, order, order), jnp.bfloat16)],
+        compiler_params=pltpu.CompilerParams(vmem_limit_bytes=40 * 2**20),
+        cost_estimate=pl.CostEstimate(
+            flops=flops, bytes_accessed=16 * count * order**2, transcendentals=0
+        ),
+    )(*operands)
 
 
 def passed_along(value, axis, by):
@@ -142,42 +209,22 @@
     return joined.reshape((2 * even_rows.shape[0],) + even_rows.shape[1:])
 
 
-def transposed(blocks):
-    return jnp.swapaxes(blocks, -1, -2)
-
-
 def gram_term(former, latter):
     return jnp.einsum("rmka,rmkb->rmab", former, latter, preferred_element_type=jnp.float32)
 
 
-def solve(inverse, coupling, axes):
-    high, low = split(inverse)
-    dot = functools.partial(jnp.einsum, axes, preferred_element_type=jnp.float32)
-    return dot(high, coupling) + dot(low, coupling)
-
-
 def on_device(diag_blocks, horizontal, vertical):
-    rows, half = diag_blocks.shape[0], diag_blocks.shape[1] // 2
-    block = diag_blocks.shape[2:]
-    edge_column = passed_along(horizontal[:, -1:], "col", 1)
-    left_links = jnp.concatenate([edge_column, horizontal[:, :-1]], 1)
-    edge_row = passed_along(vertical[-1:], "row", 1)
-    upper_links = jnp.concatenate([edge_row, vertical[:-1]], 0)
-    red_factor, inverse = factored(select_colour(diag_blocks, 0).reshape((-1,) + block))
-    inverse = inverse.reshape((rows, half) + block)
-    solved = jnp.stack(
-        [
-            solve(inverse, select_colour(left_links, 0), "rmab,rmcb->rmac"),
-            solve(inverse, select_colour(upper_links, 0), "rmab,rmcb->rmac"),
-            solve(inverse, select_colour(horizontal, 0), "rmab,rmbc->rmac"),
-            solve(inverse, select_colour(vertical, 0), "rmab,rmbc->rmac"),
-        ],
-        2,
-    ).astype(jnp.bfloat16)
-    red_factor = red_factor.reshape((rows, half) + block)
+    edge_up = passed_along(vertical[-1:, :1], "row", 1)
+    ahead = passed_along(jnp.stack([horizontal[0, 0], vertical[0, 0]]), "row", -1)
+    edge_left = passed_along(horizontal[:1, -1:], "col", 1)
+    ahead_left = passed_along(edge_left, "row", -1)
+    red_factor, packed = factored(diag_blocks)
+    below_packed = passed_along(packed[:1], "row", -1)
+    solved = solved_with(own_kernel, 2, (packed, edge_left, edge_up, horizontal, vertical))
+    red_factor = red_factor[:, None]
     got_above = passed_along(solved[-1:, :, 3], "row", 1)
     above_down = jnp.concatenate([got_above, solved[:-1, :, 3]], 0)
-    got_below = passed_along(solved[:1], "row", -1)
+    got_below = solved_with(below_kernel, 1, (below_packed, ahead_left, vertical, ahead))
     below_all = jnp.concatenate([solved[1:], got_below], 0)
     got_left = passed_along(solved[1::2, -1:, 2:4], "col", 1)
     left_pair = combine_rows(

time: 129 us -> 96.9 us (0.75)
  waiting for transfers between devices: 61.4 us -> 28.6 us
  Pallas kernels: 31.6 us -> 36.9 us
  starting transfers between devices: 8.9 us -> 6.58 us
  matrix products: 15.1 us -> 13.6 us
    ppermute x7 -> x9, waiting for transfers between devices: 61.4 us -> 28.6 us  [passed_along(): lax.ppermute(value, axis, [(i, (i + by) % size) for i in range(size)])]
    dot_general x8 -> x0, matrix products: 5.88 us -> none  [solve(): return dot(high, coupling) + dot(low, coupling)]
    pallas_call x1 -> x3, Pallas kernels: 31.6 us -> 36.9 us  [the longest x1 31.5 us: factored(): pl.pallas_call(factor_kernel, out_shape=(jax.ShapeDtypeStruct(whole, jnp....]
    dot_general x10, matrix products: 9.18 us -> 13.6 us  [gram_term(): jnp.einsum('rmka,rmkb->rmab', former, latter, preferred_element_type=jnp....]
    ppermute x7 -> x9, starting transfers between devices: 8.9 us -> 6.58 us  [passed_along(): lax.ppermute(value, axis, [(i, (i + by) % size) for i in range(size)])]
    another operation x0 -> x1, local copies, waits for them, and re-layouts: none -> 1.81 us  [on_device(): jnp.stack([horizontal[0, 0], vertical[0, 0]])]
    slice x3, local copies, waits for them, and re-layouts: 2.24 us -> 0.54 us  [the longest x1 0.36 us: on_device(): solved[0::2, :, 2:4]]
    unnamed x7 -> x13, local copies, waits for them, and re-layouts: 3.58 us -> 2.51 us
  transfers between devices with their start and end apart: 7 -> 9, of which waited for: 2 -> 4; matrix products, arithmetic and copies ran while one was open for 7% -> 12% of each run, Pallas kernels for 25% -> 39%
where the time goes in v2:
time: 96.9 us; the launch traced here: 95.3 us
  Pallas kernels  36.9 us (38%)
  waiting for transfers between devices  28.6 us (30%)
  matrix products  13.6 us (14%)
  starting transfers between devices  6.58 us (7%)
  local copies, waits for them, and re-layouts  6.21 us (6%)
  other arithmetic  2.44 us (3%)
    pallas_call x1, Pallas kernels, factored(): pl.pallas_call(factor_kernel, out_shape=(jax.ShapeDtypeStruct(whole, jnp....  31.5 us
    ppermute x9, waiting for transfers between devices, passed_along(): lax.ppermute(value, axis, [(i, (i + by) % size) for i in range(size)])  28.6 us
    dot_general x10, matrix products, gram_term(): jnp.einsum('rmka,rmkb->rmab', former, latter, preferred_element_type=jnp....  13.6 us
    ppermute x9, starting transfers between devices, passed_along(): lax.ppermute(value, axis, [(i, (i + by) % size) for i in range(size)])  6.58 us
    pallas_call x2, Pallas kernels, solved_with(): pl.pallas_call(kernel, out_shape=jax.ShapeDtypeStruct((count, 1, 4, order...  5.42 us
    unnamed x13, local copies, waits for them, and re-layouts  2.51 us
  transfers between devices with their start and end apart: 9, of which 4 were waited for; matrix products, arithmetic and copies ran while one was open for 12% of the time, Pallas kernels for 39%

profile of v2, /device:TPU:27, one launch (start us, length us, event | category | flops | bytes accessed | tf_op | source)
XLA Modules:
  0.0 95.3 jit_solution(4029797215530310380)
XLA Ops:
  0.6 0.0 copy-start.1
  0.6 1.8 %slice_bitcast_fusion.14 = (bf16[1,512,512]{2,1,0:T(8,128)(2,1)S(1)}, bf16[1,1,512,512]{3,2,1,0:T(8,128)(2,1)S(1)}, bf16[1,1,512,512]{3,2,1,0:T(8,128)(2,1)S(1)}, bf16[1,512,512]{2,1,0:T(8,128)(2,1)S(1)}) fusion(bf16[2,2,512,512]{3,2,1,0:T(8,128)(2,1)} %up.1, bf16[2,2,512,512]{3,2,1,0:T(8,128)(2,1)} %horizontal.1), kind=kLoop, calls=%fused_computation.48 | loop fusion | bytes 4194304 | tf_op jit(solution)/shard_map/stack;squeeze | solution.py:218
  2.5 1.8 %collective-permute-start = (bf16[1,1,512,512]{3,2,1,0:T(8,128)(2,1)S(1)}, bf16[1,1,512,512]{3,2,1,0:T(8,128)(2,1)S(1)}, u32[]{:S(2)}, u32[]{:S(2)}) collective-permute-start(bf16[1,1,512,512]{3,2,1,0:T(8,128)(2,1)S(1)} %get-tuple-element.24), channel_id=1, source_target_pairs={{0,1},{1,2},{2,3},{3,4},{4,5},{5,6},{6,7},{7,0},{8,9},{9,10},{10,1... | collective-permute-start | bytes 1572872 | tf_op jit(solution)/shard_map/ppermute | solution.py:195
  4.3 0.0 collective-permute-start.1
  4.3 0.1 pad_maximum_fusion.2
  4.4 0.0 copy-start
  4.4 0.0 copy-start.2
  4.4 1.5 %collective-permute-start.5 = (bf16[2,512,512]{2,1,0:T(8,128)(2,1)S(1)}, bf16[2,512,512]{2,1,0:T(8,128)(2,1)S(1)}, u32[]{:S(2)}, u32[]{:S(2)}) collective-permute-start(bf16[2,512,512]{2,1,0:T(8,128)(2,1)S(1)} %pad_maximum_fusion.2), channel_id=1, source_target_pairs={{0,24},{8,0},{16,8},{24,16},{1,25},{9,1},{17,9},{25,17},{2,26},{10... | collective-permute-start | bytes 3145736 | tf_op jit(solution)/shard_map/ppermute | solution.py:195
  5.9 0.0 copy-done.1
  5.9 31.5 %shard_map.58 = (f32[2,512,512]{2,1,0:T(8,128)}, bf16[2,2,10,128,128]{4,3,2,1,0:T(8,128)(2,1)S(1)}) custom-call(f32[2,2,512,512]{3,2,1,0:T(8,128)S(1)} %copy-done.1), custom_call_target="tpu_custom_call" | custom-call | flops 20000000000 | bytes 12582912 | tf_op jit(solution)/shard_map/pallas_call | solution.py:123
  37.4 0.1 slice.81
  37.5 0.2 collective-permute-start.3
  37.7 0.0 collective-permute-done.edge_left
  37.7 2.1 %collective-permute-done.1.edge_up = bf16[1,1,512,512]{3,2,1,0:T(8,128)(2,1)S(1)} collective-permute-done((bf16[1,1,512,512]{3,2,1,0:T(8,128)(2,1)S(1)}, bf16[1,1,512,512]{3,2,1,0:T(8,128)(2,1)S(1)}, u32[]{:S(2)}, u32[]{:S(2)}) %collective-permute-start.1) | collective-permute-done | bytes 524320 | tf_op jit(solution)/shard_map/ppermute | solution.py:195
  39.8 0.0 copy-done
  39.8 0.0 copy-done.2
  39.8 3.6 %shard_map.59 = bf16[2,1,4,512,512]{4,3,2,1,0:T(8,128)(2,1)S(1)} custom-call(bf16[2,2,10,128,128]{4,3,2,1,0:T(8,128)(2,1)S(1)} %get-tuple-element.6.packed, bf16[1,1,512,512]{3,2,1,0:T(8,128)(2,1)S(1)} %collective-permute-done.edge_left, bf16[1,1,512,512]{3,2,1,0:T(8,128)(2,1)S(1)} %collective-permute-done.1.edge_up, bf16[2,2,512,512]{3,2,1,0:T(8,128)(2,1)S(1)} %copy-done.2, ...), custom_call_target="tpu_custom_call" | custom-call | flops 3221225472 | bytes 8388608 | tf_op jit(solution)/shard_map/pallas_call | solution.py:180
  43.4 1.2 %slice_bitcast_fusion.13 = (bf16[1,1,512,512]{3,2,1,0:T(8,128)(2,1)}, bf16[1,1,1,512,512]{4,3,2,1,0:T(8,128)(2,1)S(1)}, bf16[1,1,512,512]{3,2,1,0:T(8,128)(2,1)}, bf16[1,1,512,512]{3,2,1,0:T(8,128)(2,1)}) fusion(bf16[2,1,4,512,512]{4,3,2,1,0:T(8,128)(2,1)S(1)} %shard_map.59), kind=kLoop, calls=%fused_computation.47 | loop fusion | bytes 4194304 | tf_op jit(solution)/shard_map/squeeze | solution.py:225
  44.6 0.0 copy-start.3
  44.6 0.0 collective-permute-start.7
  44.6 0.2 collective-permute-start.4
  44.8 0.4 fusion.34
  45.2 1.0 %collective-permute-start.8 = (bf16[1,1,2,512,512]{4,3,2,1,0:T(8,128)(2,1)S(1)}, bf16[1,1,2,512,512]{4,3,2,1,0:T(8,128)(2,1)}, u32[]{:S(2)}, u32[]{:S(2)}) collective-permute-start(bf16[1,1,2,512,512]{4,3,2,1,0:T(8,128)(2,1)S(1)} %get-tuple-element.10), channel_id=1, source_target_pairs={{0,7},{1,0},{2,1},{3,2},{4,3},{5,4},{6,5},{7,6},{8,15},{9,8},{10,9... | collective-permute-start | bytes 3145736 | tf_op jit(solution)/shard_map/ppermute | solution.py:195
  46.1 9.9 %collective-permute-done.3.packed = bf16[1,2,10,128,128]{4,3,2,1,0:T(8,128)(2,1)S(1)} collective-permute-done((bf16[1,2,10,128,128]{4,3,2,1,0:T(8,128)(2,1)S(1)}, bf16[1,2,10,128,128]{4,3,2,1,0:T(8,128)(2,1)S(1)}, u32[]{:S(2)}, u32[]{:S(2)}) %collective-permute-start.3) | collective-permute-done | bytes 655392 | tf_op jit(solution)/shard_map/ppermute | solution.py:195
  56.1 0.0 collective-permute-start.2
  56.1 0.2 slice_bitcast_fusion.8
  56.3 0.1 slice.100
  56.4 0.0 collective-permute-done.5.right
  56.4 1.9 %collective-permute-start.6 = (bf16[1,1,2,512,512]{4,3,2,1,0:T(8,128)(2,1)S(1)}, bf16[1,1,2,512,512]{4,3,2,1,0:T(8,128)(2,1)S(1)}, u32[]{:S(2)}, u32[]{:S(2)}) collective-permute-start(bf16[1,1,2,512,512]{4,3,2,1,0:T(8,128)(2,1)S(1)} %get-tuple-element.13), channel_id=1, source_target_pairs={{0,1},{1,2},{2,3},{3,4},{4,5},{5,6},{6,7},{7,0},{8,9},{9,10},{10,1... | collective-permute-start | bytes 3145736 | tf_op jit(solution)/shard_map/ppermute | solution.py:195
  58.3 9.1 %collective-permute-done.4.left = bf16[1,1,512,512]{3,2,1,0:T(8,128)(2,1)S(1)} collective-permute-done((bf16[1,1,512,512]{3,2,1,0:T(8,128)(2,1)S(1)}, bf16[1,1,512,512]{3,2,1,0:T(8,128)(2,1)S(1)}, u32[]{:S(2)}, u32[]{:S(2)}) %collective-permute-start.4) | collective-permute-done | bytes 524320 | tf_op jit(solution)/shard_map/ppermute | solution.py:195
  67.4 1.8 %shard_map.60 = bf16[1,1,4,512,512]{4,3,2,1,0:T(8,128)(2,1)S(1)} custom-call(bf16[1,2,10,128,128]{4,3,2,1,0:T(8,128)(2,1)S(1)} %collective-permute-done.3.packed, bf16[1,1,512,512]{3,2,1,0:T(8,128)(2,1)S(1)} %collective-permute-done.4.left, bf16[2,2,512,512]{3,2,1,0:T(8,128)(2,1)S(1)} %copy-done, bf16[2,512,512]{2,1,0:T(8,128)(2,1)S(1)} %collective-permute-done.5.right), custom_call_target="tpu_custom_call" | custom-call | flops 1610612736 | bytes 4194304 | tf_op jit(solution)/shard_map/pallas_call | solution.py:180
  69.2 0.0 copy-start.5
  69.2 0.0 collective-permute-done.7
  69.2 0.0 copy-done.3
  69.2 2.0 %fusion.26 = f32[2,512,512]{2,1,0:T(8,128)S(1)} fusion(bf16[1,1,1,512,512]{4,3,2,1,0:T(8,128)(2,1)S(1)} %get-tuple-element.15, bf16[1,1,1,512,512]{4,3,2,1,0:T(8,128)(2,1)} %bitcast.18), kind=kOutput, calls=%fused_computation.50 | convolution fusion | flops 537395200 | bytes 3145728 | tf_op jit(solution)/shard_map/rmka,rmkb->rmab/dot_general | solution.py:213
  71.3 7.4 %collective-permute-done.2 = bf16[1,1,512,512]{3,2,1,0:T(8,128)(2,1)} collective-permute-done((bf16[1,1,512,512]{3,2,1,0:T(8,128)(2,1)}, bf16[1,1,512,512]{3,2,1,0:T(8,128)(2,1)}, u32[]{:S(2)}, u32[]{:S(2)}) %collective-permute-start.2) | collective-permute-done | bytes 524320 | tf_op jit(solution)/shard_map/ppermute | solution.py:195
  78.7 0.0 copy-done.5
  78.7 2.0 %fusion.22 = f32[2,512,512]{2,1,0:T(8,128)S(1)} fusion(bf16[1,1,512,512]{3,2,1,0:T(8,128)(2,1)S(1)} %copy-done.5, bf16[1,1,512,512]{3,2,1,0:T(8,128)(2,1)} %collective-permute-done.2), kind=kOutput, calls=%fused_computation.39 | convolution fusion | flops 537395200 | bytes 3145728 | tf_op jit(solution)/shard_map/rmka,rmkb->rmab/dot_general | solution.py:213
  80.6 0.1 fusion.13
  80.7 0.8 fusion.3
  81.5 0.0 collective-permute-done.8
  81.5 0.0 copy-start.4
  81.5 1.5 %maximum_bitcast_fusion.2 = bf16[2,1,2,512,512]{4,3,2,0,1:T(8,128)(2,1)S(1)} fusion(bf16[1,1,1,2,512,512]{5,4,3,2,1,0:T(8,128)(2,1)S(1)} %get-tuple-element.12, bf16[1,1,1,2,512,512]{5,4,3,2,1,0:T(8,128)(2,1)} %bitcast.22), kind=kLoop, calls=%fused_computation.11 | loop fusion | flops 1048576 | bytes 4194304 | tf_op jit(solution)/shard_map/reshape | solution.py:209
  83.0 0.0 copy-done.4
  83.0 1.8 %fusion.2 = bf16[2,1,1,512,512]{4,3,0,2,1:T(8,128)(2,1)S(1)} fusion(bf16[2,1,2,512,512]{4,3,2,0,1:T(8,128)(2,1)S(1)} %maximum_bitcast_fusion.2, bf16[1,1,1,512,512]{4,3,2,1,0:T(8,128)(2,1)S(1)} %copy-done.4, bf16[1,1,1,512,512]{4,3,2,1,0:T(8,128)(2,1)} %bitcast.18), kind=kOutput, calls=%fused_computation.16 | convolution fusion | flops 538443776 | bytes 3145728 | tf_op jit(solution)/shard_map/rmka,rmkb->rmab/dot_general | solution.py:213
  84.8 1.8 %fusion.21 = f32[2,512,512]{2,1,0:T(8,128)S(1)} fusion(bf16[2,1,2,512,512]{4,3,2,0,1:T(8,128)(2,1)S(1)} %maximum_bitcast_fusion.2, bf16[1,1,1,512,512]{4,3,2,1,0:T(8,128)(2,1)S(1)} %copy-done.4, bf16[1,1,1,512,512]{4,3,2,1,0:T(8,128)(2,1)} %bitcast.18), kind=kOutput, calls=%fused_computation.33 | convolution fusion | flops 537395200 | bytes 4194304 | tf_op jit(solution)/shard_map/rmka,rmkb->rmab/dot_general | solution.py:213
  86.6 0.0 collective-permute-done.6
  86.6 0.2 maximum_bitcast_fusion.1
  86.8 0.8 fusion.20
  87.6 0.8 fusion.25
  88.4 0.8 fusion.5
  89.1 0.8 fusion.4
  89.9 0.6 pad_maximum_fusion
  90.5 2.5 %copy.19 = bf16[2,1,4,512,512]{4,3,2,1,0:T(8,128)(2,1)} copy(bf16[2,1,4,512,512]{4,3,0,2,1:T(8,128)(2,1)S(1)} %pad_maximum_fusion) | data formatting | bytes 8388608
  93.0 2.3 %fusion.1 = f32[2,1,512,512]{3,2,1,0:T(8,128)} fusion(f32[1,1,1,512,512]{4,3,1,2,0:T(8,128)S(1)} %get-tuple-element.19, f32[1,1,1,512,512]{4,3,1,2,0:T(8,128)S(1)} %get-tuple-element.18, f32[2,512,512]{2,1,0:T(8,128)S(1)} %fusion.26, f32[2,512,512]{2,1,0:T(8,128)S(1)} %fusion.25, f32[2,512,512]{2,1,0:T(8,128)S(1)} %fusion.22, ...), kind=kOutput, calls=%fused_computation.9 | convolution fusion | flops 539492352 | bytes 11534336 | tf_op jit(solution)/shard_map/rmka,rmkb->rmab/dot_general | solution.py:213
Async XLA Ops:
  0.6 5.3 %copy-start.1 = (f32[2,2,512,512]{3,2,1,0:T(8,128)S(1)}, f32[2,2,512,512]{3,2,1,0:T(8,128)}, u32[]{:S(2)}) copy-start(f32[2,2,512,512]{3,2,1,0:T(8,128)} %diag.1) | copy-start | bytes 12582916
  2.5 35.2 %collective-permute-start = (bf16[1,1,512,512]{3,2,1,0:T(8,128)(2,1)S(1)}, bf16[1,1,512,512]{3,2,1,0:T(8,128)(2,1)S(1)}, u32[]{:S(2)}, u32[]{:S(2)}) collective-permute-start(bf16[1,1,512,512]{3,2,1,0:T(8,128)(2,1)S(1)} %get-tuple-element.24), channel_id=1, source_target_pairs={{0,1},{1,2},{2,3},{3,4},{4,5},{5,6},{6,7},{7,0},{8,9},{9,10},{10,1... | collective-permute-start | bytes 1572872 | tf_op jit(solution)/shard_map/ppermute | solution.py:195
  4.3 35.5 %collective-permute-start.1 = (bf16[1,1,512,512]{3,2,1,0:T(8,128)(2,1)S(1)}, bf16[1,1,512,512]{3,2,1,0:T(8,128)(2,1)S(1)}, u32[]{:S(2)}, u32[]{:S(2)}) collective-permute-start(bf16[1,1,512,512]{3,2,1,0:T(8,128)(2,1)S(1)} %get-tuple-element.23), channel_id=1, source_target_pairs={{0,8},{8,16},{16,24},{24,0},{1,9},{9,17},{17,25},{25,1},{2,10},{10... | collective-permute-start | bytes 1572872 | tf_op jit(solution)/shard_map/ppermute | solution.py:195
  4.4 35.4 %copy-start = (bf16[2,2,512,512]{3,2,1,0:T(8,128)(2,1)S(1)}, bf16[2,2,512,512]{3,2,1,0:T(8,128)(2,1)}, u32[]{:S(2)}) copy-start(bf16[2,2,512,512]{3,2,1,0:T(8,128)(2,1)} %up.1) | copy-start | bytes 6291460
  4.4 35.4 %copy-start.2 = (bf16[2,2,512,512]{3,2,1,0:T(8,128)(2,1)S(1)}, bf16[2,2,512,512]{3,2,1,0:T(8,128)(2,1)}, u32[]{:S(2)}) copy-start(bf16[2,2,512,512]{3,2,1,0:T(8,128)(2,1)} %horizontal.1) | copy-start | bytes 6291460
  4.4 52.0 %collective-permute-start.5 = (bf16[2,512,512]{2,1,0:T(8,128)(2,1)S(1)}, bf16[2,512,512]{2,1,0:T(8,128)(2,1)S(1)}, u32[]{:S(2)}, u32[]{:S(2)}) collective-permute-start(bf16[2,512,512]{2,1,0:T(8,128)(2,1)S(1)} %pad_maximum_fusion.2), channel_id=1, source_target_pairs={{0,24},{8,0},{16,8},{24,16},{1,25},{9,1},{17,9},{25,17},{2,26},{10... | collective-permute-start | bytes 3145736 | tf_op jit(solution)/shard_map/ppermute | solution.py:195
  37.5 18.6 %collective-permute-start.3 = (bf16[1,2,10,128,128]{4,3,2,1,0:T(8,128)(2,1)S(1)}, bf16[1,2,10,128,128]{4,3,2,1,0:T(8,128)(2,1)S(1)}, u32[]{:S(2)}, u32[]{:S(2)}) collective-permute-start(bf16[1,2,10,128,128]{4,3,2,1,0:T(8,128)(2,1)S(1)} %slice.81), channel_id=1, source_target_pairs={{0,24},{8,0},{16,8},{24,16},{1,25},{9,1},{17,9},{25,17},{2,26},{10... | collective-permute-start | bytes 1966088 | tf_op jit(solution)/shard_map/ppermute | solution.py:195
  44.6 24.6 %copy-start.3 = (bf16[1,1,1,512,512]{4,3,2,1,0:T(8,128)(2,1)}, bf16[1,1,1,512,512]{4,3,2,1,0:T(8,128)(2,1)S(1)}, u32[]{:S(2)}) copy-start(bf16[1,1,1,512,512]{4,3,2,1,0:T(8,128)(2,1)S(1)} %get-tuple-element.15) | copy-start | bytes 1572868
  44.6 24.6 %collective-permute-start.7 = (bf16[1,1,512,512]{3,2,1,0:T(8,128)(2,1)}, bf16[1,1,512,512]{3,2,1,0:T(8,128)(2,1)}, u32[]{:S(2)}, u32[]{:S(2)}) collective-permute-start(bf16[1,1,512,512]{3,2,1,0:T(8,128)(2,1)} %get-tuple-element.16), channel_id=1, source_target_pairs={{0,7},{1,0},{2,1},{3,2},{4,3},{5,4},{6,5},{7,6},{8,15},{9,8},{10,9... | collective-permute-start | bytes 1572872 | tf_op jit(solution)/shard_map/ppermute | solution.py:195
  44.6 22.8 %collective-permute-start.4 = (bf16[1,1,512,512]{3,2,1,0:T(8,128)(2,1)S(1)}, bf16[1,1,512,512]{3,2,1,0:T(8,128)(2,1)S(1)}, u32[]{:S(2)}, u32[]{:S(2)}) collective-permute-start(bf16[1,1,512,512]{3,2,1,0:T(8,128)(2,1)S(1)} %collective-permute-done.edge_left), channel_id=1, source_target_pairs={{0,24},{8,0},{16,8},{24,16},{1,25},{9,1},{17,9},{25,17},{2,26},{10... | collective-permute-start | bytes 1572872 | tf_op jit(solution)/shard_map/ppermute | solution.py:195
  45.2 36.3 %collective-permute-start.8 = (bf16[1,1,2,512,512]{4,3,2,1,0:T(8,128)(2,1)S(1)}, bf16[1,1,2,512,512]{4,3,2,1,0:T(8,128)(2,1)}, u32[]{:S(2)}, u32[]{:S(2)}) collective-permute-start(bf16[1,1,2,512,512]{4,3,2,1,0:T(8,128)(2,1)S(1)} %get-tuple-element.10), channel_id=1, source_target_pairs={{0,7},{1,0},{2,1},{3,2},{4,3},{5,4},{6,5},{7,6},{8,15},{9,8},{10,9... | collective-permute-start | bytes 3145736 | tf_op jit(solution)/shard_map/ppermute | solution.py:195
  56.1 22.6 %collective-permute-start.2 = (bf16[1,1,512,512]{3,2,1,0:T(8,128)(2,1)}, bf16[1,1,512,512]{3,2,1,0:T(8,128)(2,1)}, u32[]{:S(2)}, u32[]{:S(2)}) collective-permute-start(bf16[1,1,512,512]{3,2,1,0:T(8,128)(2,1)} %get-tuple-element.14), channel_id=1, source_target_pairs={{0,8},{8,16},{16,24},{24,0},{1,9},{9,17},{17,25},{25,1},{2,10},{10... | collective-permute-start | bytes 1572872 | tf_op jit(solution)/shard_map/ppermute | solution.py:195
  56.4 30.2 %collective-permute-start.6 = (bf16[1,1,2,512,512]{4,3,2,1,0:T(8,128)(2,1)S(1)}, bf16[1,1,2,512,512]{4,3,2,1,0:T(8,128)(2,1)S(1)}, u32[]{:S(2)}, u32[]{:S(2)}) collective-permute-start(bf16[1,1,2,512,512]{4,3,2,1,0:T(8,128)(2,1)S(1)} %get-tuple-element.13), channel_id=1, source_target_pairs={{0,1},{1,2},{2,3},{3,4},{4,5},{5,6},{6,7},{7,0},{8,9},{9,10},{10,1... | collective-permute-start | bytes 3145736 | tf_op jit(solution)/shard_map/ppermute | solution.py:195
  69.2 9.5 %copy-start.5 = (bf16[1,1,512,512]{3,2,1,0:T(8,128)(2,1)S(1)}, bf16[1,1,512,512]{3,2,1,0:T(8,128)(2,1)}, u32[]{:S(2)}) copy-start(bf16[1,1,512,512]{3,2,1,0:T(8,128)(2,1)} %get-tuple-element.17) | copy-start | bytes 1572868
  81.5 1.5 %copy-start.4 = (bf16[1,1,1,512,512]{4,3,2,1,0:T(8,128)(2,1)S(1)}, bf16[1,1,1,512,512]{4,3,2,1,0:T(8,128)(2,1)}, u32[]{:S(2)}) copy-start(bf16[1,1,1,512,512]{4,3,2,1,0:T(8,128)(2,1)} %copy-done.3) | copy-start | bytes 1572868

commit v3 on v2

--- a/solution.py
+++ b/solution.py
@@ -195,6 +195,16 @@
     return lax.ppermute(value, axis, [(i, (i + by) % size) for i in range(size)])
 
 
+def passed_diagonally(value):
+    rows, columns = lax.axis_size("row"), lax.axis_size("col")
+    pairs = [
+        (r * columns + c, (r - 1) % rows * columns + (c + 1) % columns)
+        for r in range(rows)
+        for c in range(columns)
+    ]
+    return lax.ppermute(value, ("row", "col"), pairs)
+
+
 def select_colour(blocks, parity):
     grid_rows = blocks.shape[0]
     grid_columns = blocks.shape[1]
@@ -217,7 +227,7 @@
     edge_up = passed_along(vertical[-1:, :1], "row", 1)
     ahead = passed_along(jnp.stack([horizontal[0, 0], vertical[0, 0]]), "row", -1)
     edge_left = passed_along(horizontal[:1, -1:], "col", 1)
-    ahead_left = passed_along(edge_left, "row", -1)
+    ahead_left = passed_diagonally(horizontal[:1, -1:])
     red_factor, packed = factored(diag_blocks)
     below_packed = passed_along(packed[:1], "row", -1)
     solved = solved_with(own_kernel, 2, (packed, edge_left, edge_up, horizontal, vertical))

time: 96.9 us -> 98.8 us (1.020)
  waiting for transfers between devices: 28.6 us -> 33.4 us
  matrix products: 13.6 us -> 9.2 us
  starting transfers between devices: 6.58 us -> 9.4 us
  other arithmetic: 2.44 us -> 1.16 us
    ppermute x9 -> x8, waiting for transfers between devices: 28.6 us -> 33.4 us  [passed_along(): lax.ppermute(value, axis, [(i, (i + by) % size) for i in range(size)])]
    dot_general x10, matrix products: 13.6 us -> 9.2 us  [gram_term(): jnp.einsum('rmka,rmkb->rmab', former, latter, preferred_element_type=jnp....]
    ppermute x0 -> x1, starting transfers between devices: none -> 1.71 us  [passed_diagonally(): return lax.ppermute(value, ('row', 'col'), pairs)]
    reshape x2, other arithmetic: 1.67 us -> 0.39 us  [combine_rows(): return joined.reshape((2 * even_rows.shape[0],) + even_rows.shape[1:])]
    ppermute x9 -> x8, starting transfers between devices: 6.58 us -> 7.69 us  [passed_along(): lax.ppermute(value, axis, [(i, (i + by) % size) for i in range(size)])]
    unnamed x13 -> x9, local copies, waits for them, and re-layouts: 2.51 us -> 2.5 us
  transfers between devices with their start and end apart: 9 -> 9, of which waited for: 4 -> 4; matrix products, arithmetic and copies ran while one was open for 12% -> 8% of each run, Pallas kernels for 39% -> 38%
where the time goes in v3:
time: 98.8 us; the launch traced here: 97.2 us
  Pallas kernels  36.9 us (37%)
  waiting for transfers between devices  33.4 us (34%)
  starting transfers between devices  9.4 us (10%)
  matrix products  9.2 us (9%)
  local copies, waits for them, and re-layouts  6.2 us (6%)
  other arithmetic  1.16 us (1%)
    ppermute x8, waiting for transfers between devices, passed_along(): lax.ppermute(value, axis, [(i, (i + by) % size) for i in range(size)])  33.4 us
    pallas_call x1, Pallas kernels, factored(): pl.pallas_call(factor_kernel, out_shape=(jax.ShapeDtypeStruct(whole, jnp....  31.5 us
    dot_general x10, matrix products, gram_term(): jnp.einsum('rmka,rmkb->rmab', former, latter, preferred_element_type=jnp....  9.2 us
    ppermute x8, starting transfers between devices, passed_along(): lax.ppermute(value, axis, [(i, (i + by) % size) for i in range(size)])  7.69 us
    pallas_call x2, Pallas kernels, solved_with(): pl.pallas_call(kernel, out_shape=jax.ShapeDtypeStruct((count, 1, 4, order...  5.43 us
    unnamed x9, local copies, waits for them, and re-layouts  2.5 us
  transfers between devices with their start and end apart: 9, of which 4 were waited for; matrix products, arithmetic and copies ran while one was open for 8% of the time, Pallas kernels for 38%

profile of v3, /device:TPU:27, one launch (start us, length us, event | category | flops | bytes accessed | tf_op | source)
XLA Modules:
  0.0 97.2 jit_solution(17020462997751092907)
XLA Ops:
  0.6 0.0 copy-start.1
  0.6 1.8 %slice_bitcast_fusion.16 = (bf16[1,512,512]{2,1,0:T(8,128)(2,1)S(1)}, bf16[1,1,512,512]{3,2,1,0:T(8,128)(2,1)S(1)}, bf16[1,1,512,512]{3,2,1,0:T(8,128)(2,1)S(1)}, bf16[1,512,512]{2,1,0:T(8,128)(2,1)S(1)}) fusion(bf16[2,2,512,512]{3,2,1,0:T(8,128)(2,1)} %up.1, bf16[2,2,512,512]{3,2,1,0:T(8,128)(2,1)} %horizontal.1), kind=kLoop, calls=%fused_computation.48 | loop fusion | bytes 4194304 | tf_op jit(solution)/shard_map/stack;squeeze | solution.py:228
  2.5 1.7 %collective-permute-start.4 = (bf16[1,1,512,512]{3,2,1,0:T(8,128)(2,1)S(1)}, bf16[1,1,512,512]{3,2,1,0:T(8,128)(2,1)S(1)}, u32[]{:S(2)}, u32[]{:S(2)}) collective-permute-start(bf16[1,1,512,512]{3,2,1,0:T(8,128)(2,1)S(1)} %get-tuple-element.24), channel_id=1, source_target_pairs={{0,25},{1,26},{2,27},{3,28},{4,29},{5,30},{6,31},{7,24},{8,1},{9,2... | collective-permute-start | bytes 1572872 | tf_op jit(solution)/shard_map/ppermute | solution.py:205
  4.2 0.2 collective-permute-start
  4.3 0.1 pad_maximum_fusion.2
  4.4 0.2 collective-permute-start.5
  4.7 3.1 %collective-permute-start.1 = (bf16[1,1,512,512]{3,2,1,0:T(8,128)(2,1)S(1)}, bf16[1,1,512,512]{3,2,1,0:T(8,128)(2,1)S(1)}, u32[]{:S(2)}, u32[]{:S(2)}) collective-permute-start(bf16[1,1,512,512]{3,2,1,0:T(8,128)(2,1)S(1)} %get-tuple-element.23), channel_id=1, source_target_pairs={{0,8},{8,16},{16,24},{24,0},{1,9},{9,17},{17,25},{25,1},{2,10},{10... | collective-permute-start | bytes 1572872 | tf_op jit(solution)/shard_map/ppermute | solution.py:195
  7.8 0.0 copy-done.1
  7.8 31.5 %shard_map.58 = (f32[2,512,512]{2,1,0:T(8,128)}, bf16[2,2,10,128,128]{4,3,2,1,0:T(8,128)(2,1)S(1)}) custom-call(f32[2,2,512,512]{3,2,1,0:T(8,128)S(1)} %copy-done.1), custom_call_target="tpu_custom_call" | custom-call | flops 20000000000 | bytes 12582912 | tf_op jit(solution)/shard_map/pallas_call | solution.py:123
  39.3 0.1 slice.82
  39.3 0.1 collective-permute-start.3
  39.4 0.0 copy-start
  39.4 0.0 copy-start.2
  39.4 0.2 slice_bitcast_fusion.10
  39.6 0.0 collective-permute-done.edge_left
  39.6 12.7 %collective-permute-done.1.edge_up = bf16[1,1,512,512]{3,2,1,0:T(8,128)(2,1)S(1)} collective-permute-done((bf16[1,1,512,512]{3,2,1,0:T(8,128)(2,1)S(1)}, bf16[1,1,512,512]{3,2,1,0:T(8,128)(2,1)S(1)}, u32[]{:S(2)}, u32[]{:S(2)}) %collective-permute-start.1) | collective-permute-done | bytes 524320 | tf_op jit(solution)/shard_map/ppermute | solution.py:195
  52.3 0.0 copy-done
  52.3 0.0 copy-done.2
  52.3 3.6 %shard_map.59 = bf16[2,1,4,512,512]{4,3,2,1,0:T(8,128)(2,1)S(1)} custom-call(bf16[2,2,10,128,128]{4,3,2,1,0:T(8,128)(2,1)S(1)} %get-tuple-element.6.packed, bf16[1,1,512,512]{3,2,1,0:T(8,128)(2,1)S(1)} %collective-permute-done.edge_left, bf16[1,1,512,512]{3,2,1,0:T(8,128)(2,1)S(1)} %collective-permute-done.1.edge_up, bf16[2,2,512,512]{3,2,1,0:T(8,128)(2,1)S(1)} %copy-done.2, ...), custom_call_target="tpu_custom_call" | custom-call | flops 3221225472 | bytes 8388608 | tf_op jit(solution)/shard_map/pallas_call | solution.py:180
  55.9 0.1 slice.101
  56.1 0.4 fusion.31
  56.4 1.1 %collective-permute-start.8 = (bf16[1,1,2,512,512]{4,3,2,1,0:T(8,128)(2,1)S(1)}, bf16[1,1,2,512,512]{4,3,2,1,0:T(8,128)(2,1)S(1)}, u32[]{:S(2)}, u32[]{:S(2)}) collective-permute-start(bf16[1,1,2,512,512]{4,3,2,1,0:T(8,128)(2,1)S(1)} %get-tuple-element.10), channel_id=1, source_target_pairs={{0,7},{1,0},{2,1},{3,2},{4,3},{5,4},{6,5},{7,6},{8,15},{9,8},{10,9... | collective-permute-start | bytes 3145736 | tf_op jit(solution)/shard_map/ppermute | solution.py:195
  57.5 1.2 %slice_bitcast_fusion.13 = (bf16[1,1,512,512]{3,2,1,0:T(8,128)(2,1)}, bf16[1,1,1,512,512]{4,3,2,1,0:T(8,128)(2,1)S(1)}, bf16[1,1,512,512]{3,2,1,0:T(8,128)(2,1)}, bf16[1,1,512,512]{3,2,1,0:T(8,128)(2,1)}) fusion(bf16[2,1,4,512,512]{4,3,2,1,0:T(8,128)(2,1)S(1)} %shard_map.59), kind=kLoop, calls=%fused_computation.45 | loop fusion | bytes 4194304 | tf_op jit(solution)/shard_map/squeeze | solution.py:243
  58.7 0.0 collective-permute-start.7
  58.7 0.0 collective-permute-done.4.left
  58.7 2.6 %collective-permute-start.6 = (bf16[1,1,2,512,512]{4,3,2,1,0:T(8,128)(2,1)S(1)}, bf16[1,1,2,512,512]{4,3,2,1,0:T(8,128)(2,1)S(1)}, u32[]{:S(2)}, u32[]{:S(2)}) collective-permute-start(bf16[1,1,2,512,512]{4,3,2,1,0:T(8,128)(2,1)S(1)} %get-tuple-element.13), channel_id=1, source_target_pairs={{0,1},{1,2},{2,3},{3,4},{4,5},{5,6},{6,7},{7,0},{8,9},{9,10},{10,1... | collective-permute-start | bytes 3145736 | tf_op jit(solution)/shard_map/ppermute | solution.py:195
  61.3 5.1 %collective-permute-done.3.packed = bf16[1,2,10,128,128]{4,3,2,1,0:T(8,128)(2,1)S(1)} collective-permute-done((bf16[1,2,10,128,128]{4,3,2,1,0:T(8,128)(2,1)S(1)}, bf16[1,2,10,128,128]{4,3,2,1,0:T(8,128)(2,1)S(1)}, u32[]{:S(2)}, u32[]{:S(2)}) %collective-permute-start.3) | collective-permute-done | bytes 655392 | tf_op jit(solution)/shard_map/ppermute | solution.py:195
  66.4 0.4 collective-permute-start.2
  66.8 0.0 collective-permute-done.5.right
  66.8 1.8 %shard_map.60 = bf16[1,1,4,512,512]{4,3,2,1,0:T(8,128)(2,1)S(1)} custom-call(bf16[1,2,10,128,128]{4,3,2,1,0:T(8,128)(2,1)S(1)} %collective-permute-done.3.packed, bf16[1,1,512,512]{3,2,1,0:T(8,128)(2,1)S(1)} %collective-permute-done.4.left, bf16[2,2,512,512]{3,2,1,0:T(8,128)(2,1)S(1)} %copy-done, bf16[2,512,512]{2,1,0:T(8,128)(2,1)S(1)} %collective-permute-done.5.right), custom_call_target="tpu_custom_call" | custom-call | flops 1610612736 | bytes 4194304 | tf_op jit(solution)/shard_map/pallas_call | solution.py:180
  68.6 0.1 fusion.11
  68.7 0.8 fusion.8
  69.5 0.8 fusion.3
  70.3 0.0 copy-start.3
  70.3 0.8 fusion.32
  71.0 9.3 %collective-permute-done.2 = bf16[1,1,512,512]{3,2,1,0:T(8,128)(2,1)S(1)} collective-permute-done((bf16[1,1,512,512]{3,2,1,0:T(8,128)(2,1)}, bf16[1,1,512,512]{3,2,1,0:T(8,128)(2,1)S(1)}, u32[]{:S(2)}, u32[]{:S(2)}) %collective-permute-start.2) | collective-permute-done | bytes 524320 | tf_op jit(solution)/shard_map/ppermute | solution.py:195
  80.3 0.0 copy-done.3
  80.3 0.8 fusion.20
  81.1 0.8 fusion.16
  81.8 0.0 collective-permute-done.8
  81.8 0.2 maximum_bitcast_fusion.2
  82.0 6.4 %collective-permute-done.7 = bf16[1,1,512,512]{3,2,1,0:T(8,128)(2,1)S(1)} collective-permute-done((bf16[1,1,512,512]{3,2,1,0:T(8,128)(2,1)}, bf16[1,1,512,512]{3,2,1,0:T(8,128)(2,1)S(1)}, u32[]{:S(2)}, u32[]{:S(2)}) %collective-permute-start.7) | collective-permute-done | bytes 524320 | tf_op jit(solution)/shard_map/ppermute | solution.py:195
  88.5 0.8 fusion.2
  89.2 0.8 fusion.4
  90.0 0.0 collective-permute-done.6
  90.0 0.2 maximum_bitcast_fusion.1
  90.2 0.8 fusion.23
  91.0 0.8 fusion.5
  91.8 0.6 pad_maximum_fusion
  92.3 2.5 %copy.19 = bf16[2,1,4,512,512]{4,3,2,1,0:T(8,128)(2,1)} copy(bf16[2,1,4,512,512]{4,3,0,2,1:T(8,128)(2,1)S(1)} %pad_maximum_fusion) | data formatting | bytes 8388608
  94.8 2.4 %fusion.1 = f32[2,1,512,512]{3,2,1,0:T(8,128)} fusion(f32[1,1,1,512,512]{4,3,1,2,0:T(8,128)S(1)} %get-tuple-element.19, f32[1,1,1,512,512]{4,3,1,2,0:T(8,128)S(1)} %get-tuple-element.18, f32[2,512,512]{2,1,0:T(8,128)S(1)} %fusion.23, f32[2,512,512]{2,1,0:T(8,128)S(1)} %fusion.20, f32[2,512,512]{2,1,0:T(8,128)S(1)} %fusion.32, ...), kind=kOutput, calls=%fused_computation.9 | convolution fusion | flops 540016640 | bytes 11534336 | tf_op jit(solution)/shard_map/rmka,rmkb->rmab/dot_general | solution.py:223
Async XLA Ops:
  0.6 7.1 %copy-start.1 = (f32[2,2,512,512]{3,2,1,0:T(8,128)S(1)}, f32[2,2,512,512]{3,2,1,0:T(8,128)}, u32[]{:S(2)}) copy-start(f32[2,2,512,512]{3,2,1,0:T(8,128)} %diag.1) | copy-start | bytes 12582916
  2.5 56.2 %collective-permute-start.4 = (bf16[1,1,512,512]{3,2,1,0:T(8,128)(2,1)S(1)}, bf16[1,1,512,512]{3,2,1,0:T(8,128)(2,1)S(1)}, u32[]{:S(2)}, u32[]{:S(2)}) collective-permute-start(bf16[1,1,512,512]{3,2,1,0:T(8,128)(2,1)S(1)} %get-tuple-element.24), channel_id=1, source_target_pairs={{0,25},{1,26},{2,27},{3,28},{4,29},{5,30},{6,31},{7,24},{8,1},{9,2... | collective-permute-start | bytes 1572872 | tf_op jit(solution)/shard_map/ppermute | solution.py:205
  4.2 35.4 %collective-permute-start = (bf16[1,1,512,512]{3,2,1,0:T(8,128)(2,1)S(1)}, bf16[1,1,512,512]{3,2,1,0:T(8,128)(2,1)S(1)}, u32[]{:S(2)}, u32[]{:S(2)}) collective-permute-start(bf16[1,1,512,512]{3,2,1,0:T(8,128)(2,1)S(1)} %get-tuple-element.24), channel_id=1, source_target_pairs={{0,1},{1,2},{2,3},{3,4},{4,5},{5,6},{6,7},{7,0},{8,9},{9,10},{10,1... | collective-permute-start | bytes 1572872 | tf_op jit(solution)/shard_map/ppermute | solution.py:195
  4.4 62.3 %collective-permute-start.5 = (bf16[2,512,512]{2,1,0:T(8,128)(2,1)S(1)}, bf16[2,512,512]{2,1,0:T(8,128)(2,1)S(1)}, u32[]{:S(2)}, u32[]{:S(2)}) collective-permute-start(bf16[2,512,512]{2,1,0:T(8,128)(2,1)S(1)} %pad_maximum_fusion.2), channel_id=1, source_target_pairs={{0,24},{8,0},{16,8},{24,16},{1,25},{9,1},{17,9},{25,17},{2,26},{10... | collective-permute-start | bytes 3145736 | tf_op jit(solution)/shard_map/ppermute | solution.py:195
  4.7 47.6 %collective-permute-start.1 = (bf16[1,1,512,512]{3,2,1,0:T(8,128)(2,1)S(1)}, bf16[1,1,512,512]{3,2,1,0:T(8,128)(2,1)S(1)}, u32[]{:S(2)}, u32[]{:S(2)}) collective-permute-start(bf16[1,1,512,512]{3,2,1,0:T(8,128)(2,1)S(1)} %get-tuple-element.23), channel_id=1, source_target_pairs={{0,8},{8,16},{16,24},{24,0},{1,9},{9,17},{17,25},{25,1},{2,10},{10... | collective-permute-start | bytes 1572872 | tf_op jit(solution)/shard_map/ppermute | solution.py:195
  39.3 27.0 %collective-permute-start.3 = (bf16[1,2,10,128,128]{4,3,2,1,0:T(8,128)(2,1)S(1)}, bf16[1,2,10,128,128]{4,3,2,1,0:T(8,128)(2,1)S(1)}, u32[]{:S(2)}, u32[]{:S(2)}) collective-permute-start(bf16[1,2,10,128,128]{4,3,2,1,0:T(8,128)(2,1)S(1)} %slice.82), channel_id=1, source_target_pairs={{0,24},{8,0},{16,8},{24,16},{1,25},{9,1},{17,9},{25,17},{2,26},{10... | collective-permute-start | bytes 1966088 | tf_op jit(solution)/shard_map/ppermute | solution.py:195
  39.4 12.9 %copy-start = (bf16[2,2,512,512]{3,2,1,0:T(8,128)(2,1)S(1)}, bf16[2,2,512,512]{3,2,1,0:T(8,128)(2,1)}, u32[]{:S(2)}) copy-start(bf16[2,2,512,512]{3,2,1,0:T(8,128)(2,1)} %up.1) | copy-start | bytes 6291460
  39.4 12.9 %copy-start.2 = (bf16[2,2,512,512]{3,2,1,0:T(8,128)(2,1)S(1)}, bf16[2,2,512,512]{3,2,1,0:T(8,128)(2,1)}, u32[]{:S(2)}) copy-start(bf16[2,2,512,512]{3,2,1,0:T(8,128)(2,1)} %horizontal.1) | copy-start | bytes 6291460
  56.4 25.4 %collective-permute-start.8 = (bf16[1,1,2,512,512]{4,3,2,1,0:T(8,128)(2,1)S(1)}, bf16[1,1,2,512,512]{4,3,2,1,0:T(8,128)(2,1)S(1)}, u32[]{:S(2)}, u32[]{:S(2)}) collective-permute-start(bf16[1,1,2,512,512]{4,3,2,1,0:T(8,128)(2,1)S(1)} %get-tuple-element.10), channel_id=1, source_target_pairs={{0,7},{1,0},{2,1},{3,2},{4,3},{5,4},{6,5},{7,6},{8,15},{9,8},{10,9... | collective-permute-start | bytes 3145736 | tf_op jit(solution)/shard_map/ppermute | solution.py:195
  58.7 29.8 %collective-permute-start.7 = (bf16[1,1,512,512]{3,2,1,0:T(8,128)(2,1)}, bf16[1,1,512,512]{3,2,1,0:T(8,128)(2,1)S(1)}, u32[]{:S(2)}, u32[]{:S(2)}) collective-permute-start(bf16[1,1,512,512]{3,2,1,0:T(8,128)(2,1)} %get-tuple-element.14), channel_id=1, source_target_pairs={{0,7},{1,0},{2,1},{3,2},{4,3},{5,4},{6,5},{7,6},{8,15},{9,8},{10,9... | collective-permute-start | bytes 1572872 | tf_op jit(solution)/shard_map/ppermute | solution.py:195
  58.7 31.3 %collective-permute-start.6 = (bf16[1,1,2,512,512]{4,3,2,1,0:T(8,128)(2,1)S(1)}, bf16[1,1,2,512,512]{4,3,2,1,0:T(8,128)(2,1)S(1)}, u32[]{:S(2)}, u32[]{:S(2)}) collective-permute-start(bf16[1,1,2,512,512]{4,3,2,1,0:T(8,128)(2,1)S(1)} %get-tuple-element.13), channel_id=1, source_target_pairs={{0,1},{1,2},{2,3},{3,4},{4,5},{5,6},{6,7},{7,0},{8,9},{9,10},{10,1... | collective-permute-start | bytes 3145736 | tf_op jit(solution)/shard_map/ppermute | solution.py:195
  66.4 13.9 %collective-permute-start.2 = (bf16[1,1,512,512]{3,2,1,0:T(8,128)(2,1)}, bf16[1,1,512,512]{3,2,1,0:T(8,128)(2,1)S(1)}, u32[]{:S(2)}, u32[]{:S(2)}) collective-permute-start(bf16[1,1,512,512]{3,2,1,0:T(8,128)(2,1)} %get-tuple-element.17), channel_id=1, source_target_pairs={{0,8},{8,16},{16,24},{24,0},{1,9},{9,17},{17,25},{25,1},{2,10},{10... | collective-permute-start | bytes 1572872 | tf_op jit(solution)/shard_map/ppermute | solution.py:195
  70.3 10.0 %copy-start.3 = (bf16[1,1,512,512]{3,2,1,0:T(8,128)(2,1)S(1)}, bf16[1,1,512,512]{3,2,1,0:T(8,128)(2,1)}, u32[]{:S(2)}) copy-start(bf16[1,1,512,512]{3,2,1,0:T(8,128)(2,1)} %get-tuple-element.16) | copy-start | bytes 1572868
